TPU v7x, 256 devices: a whole 4x4x8 slice. The times are simulated.
256 devices in a mesh: chan: 4 (over y), slab: 64 (over x, z, core).
Axes of the slice: x: 4, y: 4, z: 8, core: 2. Of those that a mesh axis runs over, the one named last changes fastest.
Arguments:
- flux: float32 [4, 4096, 128], P('chan', 'slab'), may hold values from -6 to 6
- offsets: int32 [4096, 128], P('slab'), may hold values from 0 to 8191
- counts: int32 [4096], P('slab'), may hold values from 96 to 128
- dest_owner: int32 [4096, 1], P('slab'), may hold values from 0 to 63; in each aligned block of 64 rows (0 to 63, 64 to 127, ...) at most 2 rows name the same one
- dest_tile: int32 [4096], P('slab'), may hold values from 0 to 31
- dirty: float32 [4, 4096, 4096], P('chan', 'slab'), may hold values from -60 to 60
- psf_real: float32 [4, 8192, 8192], P('chan', None, 'slab'), may hold values from -96 to 96
- psf_imag: float32 [4, 8192, 8192], P('chan', None, 'slab'), may hold values from -96 to 96
Outputs:
- residual: float32 [4, 4096, 4096], P('chan', 'slab')
- rms_values: float32 [4], replicated
- peak_values: float32 [4], replicated
Inputs may be any that keep to these rules, and one draw needn't show every extreme that they name: `dest_owner`: among the 64 blocks of one device (aligned blocks of rows) at most 2 name the same owner, a bound that some device reaches. `counts`: slots at or beyond a block's count hold no component.
All inputs are finite; a program needn't handle non-finite values.
Results may differ from a plain program's by a relative error of at most 0.00005.
Values sent between devices are 32-bit elements; how exact they have to be, the bound alone decides.
A program may use at most 128 MiB of HBM per device.

v0:
```python
import math

import jax
import jax.numpy as jnp
from jax import lax
from jax.sharding import Mesh
from jax.sharding import PartitionSpec as P

TILE_R = 64
TILE_C = 128
SLAB = ("slab_0", "slab_1", "slab_2")


PRECISE = lax.Precision.HIGHEST


def cut_along(shard, dim, peers):
    before, after = (shard.shape[:dim], shard.shape[dim + 1 :])
    return jnp.moveaxis(shard.reshape(*before, peers, -1, *after), dim, 0)


def joined_along(pieces, dim):
    pieces = jnp.moveaxis(pieces, 0, dim)
    shape = pieces.shape
    return pieces.reshape(*shape[:dim], shape[dim] * shape[dim + 1], *shape[dim + 2 :])


def turned_blocks(pieces, axes, sequence):
    shape = [lax.axis_size(a) for a in axes]
    pieces = pieces.reshape(*shape, *pieces.shape[1:])
    for k in sequence:
        pieces = lax.all_to_all(pieces, axes[k], split_axis=k, concat_axis=k, tiled=True)
    return pieces.reshape(-1, *pieces.shape[len(axes) :])


def core_and_chips(shard, groups, sequence, split_dim, concat_dim):
    peers = lax.axis_size(groups[0]) * lax.axis_size(groups[1])
    pieces = cut_along(shard, split_dim, peers)
    return joined_along(turned_blocks(pieces, groups, sequence), concat_dim)


def sent_to_all(shard, axis):
    copies = jnp.broadcast_to(shard, (lax.axis_size(axis), *shard.shape))
    return lax.all_to_all(copies, axis, split_axis=0, concat_axis=0, tiled=True)


def taken_together(shard, axis):
    everything = sent_to_all(shard, axis)
    return jnp.sum(everything, axis=0)


def over_copies(shard, axis):
    everything = sent_to_all(shard, axis)
    return jnp.max(everything, axis=0)


def rows_first(arrays, axis, dims):
    turned = [jnp.moveaxis(a, dim, 0) for a, dim in zip(arrays, dims)]
    widths = [t[0].size for t in turned]
    both = jnp.concatenate([t.reshape(-1, w) for t, w in zip(turned, widths)], axis=1)
    whole = lax.all_gather(both, axis, axis=0, tiled=True)
    pieces = jnp.split(whole, [sum(widths[:k]) for k in range(1, len(widths))], axis=1)
    return tuple(
        (
            jnp.moveaxis(b.reshape(-1, *t.shape[1:]), 0, dim)
            for b, t, dim in zip(pieces, turned, dims)
        )
    )


def factor(length):
    levels = length.bit_length() - 1
    outer_len = 2 ** ((levels + 1) // 2)
    return (outer_len, length // outer_len)


def rotation(count_one, count_two, length, sign):
    row_ids = jnp.arange(count_one, dtype=jnp.int32)[:, None]
    col_ids = jnp.arange(count_two, dtype=jnp.int32)[None, :]
    turn_count = row_ids * col_ids % length
    angles = turn_count.astype(jnp.float32) * (2.0 * math.pi / length)
    return (jnp.cos(angles), sign * jnp.sin(angles))


def table(count_one, count_two, length, sign):
    cosine, sine = rotation(count_one, count_two, length, sign)
    first = jnp.stack([cosine, sine], axis=1)
    second = jnp.stack([-sine, cosine], axis=1)
    return jnp.stack([first, second], axis=0)


def contract(pattern, first_op, second_op):
    return jnp.einsum(pattern, first_op, second_op, precision=PRECISE)


def twiddle(values, phases):
    phase_re, phase_im = phases
    value_re = values[0]
    value_im = values[1]
    return jnp.stack(
        [value_re * phase_re - value_im * phase_im, value_re * phase_im + value_im * phase_re]
    )


def widen(phases):
    return (phases[0][:, :, None], phases[1][:, :, None])


def forward_rows(image, length):
    outer_len, inner_len = factor(length)
    row_count = image.shape[0]
    pieces = image.reshape(row_count, outer_len // 2, inner_len)
    partial_sum = contract(
        "rab,atk->trkb", pieces, table(outer_len // 2, outer_len, outer_len, -1.0)[0]
    )
    partial_sum = twiddle(partial_sum, rotation(outer_len, inner_len, length, -1.0))
    result = contract("srkb,sbtj->trjk", partial_sum, table(inner_len, inner_len, inner_len, -1.0))
    return result.reshape(2, row_count, length)


def forward_cols(values, length):
    outer_len, inner_len = factor(length)
    col_count = values.shape[2]
    pieces = values.reshape(2, outer_len // 2, inner_len, col_count)
    partial_sum = contract(
        "sabc,satk->tkbc", pieces, table(outer_len // 2, outer_len, outer_len, -1.0)
    )
    partial_sum = twiddle(partial_sum, widen(rotation(outer_len, inner_len, length, -1.0)))
    result = contract("skbc,sbtj->tjkc", partial_sum, table(inner_len, inner_len, inner_len, -1.0))
    return result.reshape(2, length, col_count)


def inverse_cols(values, length):
    outer_len, inner_len = factor(length)
    col_count = values.shape[2]
    pieces = values.reshape(2, outer_len, inner_len, col_count)
    partial_sum = contract("sabc,sate->tebc", pieces, table(outer_len, outer_len, outer_len, 1.0))
    partial_sum = twiddle(partial_sum, widen(rotation(outer_len, inner_len, length, 1.0)))
    result = contract(
        "sebc,sbtd->tdec", partial_sum, table(inner_len, inner_len // 2, inner_len, 1.0)
    )
    return result.reshape(2, length // 2, col_count) * (1.0 / length)


def inverse_rows(values, length):
    outer_len, inner_len = factor(length)
    row_count = values.shape[1]
    pieces = values.reshape(2, row_count, outer_len, inner_len)
    partial_sum = contract("srab,sate->treb", pieces, table(outer_len, outer_len, outer_len, 1.0))
    partial_sum = twiddle(partial_sum, rotation(outer_len, inner_len, length, 1.0))
    real_table = table(inner_len, inner_len // 2, inner_len, 1.0)[:, :, 0]
    real_part = contract("sreb,sbd->rde", partial_sum, real_table)
    return real_part.reshape(row_count, length // 2) * (1.0 / length)


def on_device(flux, offsets, counts, dest_owner, dest_tile, dirty, psf_real, psf_imag):
    slab_count = lax.axis_size(SLAB)
    chan_local, rows_dev, row_width = dirty.shape
    length = 2 * row_width
    blocks, comp_slots = offsets.shape
    slab_area = rows_dev * row_width
    across = row_width // TILE_C
    tile_row = dest_tile // across
    tile_col = dest_tile % across
    pixels = (
        (tile_row[:, None] * TILE_R + offsets // TILE_C) * row_width
        + tile_col[:, None] * TILE_C
        + offsets % TILE_C
    )
    live_mask = jnp.arange(comp_slots, dtype=jnp.int32)[None, :] < counts[:, None]
    weights = jnp.where(live_mask[None], flux, 0.0)
    owner_ids = dest_owner[:, 0]
    send_slots = 2 * blocks // slab_count
    owner_marks = (owner_ids[:, None] == jnp.arange(slab_count, dtype=jnp.int32)[None, :]).astype(
        jnp.int32
    )
    owner_ranks = jnp.sum((jnp.cumsum(owner_marks, axis=0) - 1) * owner_marks, axis=1)
    slot_index = owner_ids * send_slots + owner_ranks
    pixel_box = (
        jnp.zeros((slab_count * send_slots, comp_slots), jnp.int32).at[slot_index].set(pixels)
    )
    flux_box = (
        jnp.zeros((chan_local, slab_count * send_slots, comp_slots), jnp.float32)
        .at[:, slot_index]
        .set(weights)
    )
    got_pixels = lax.all_to_all(
        pixel_box.reshape(slab_count, send_slots, comp_slots),
        SLAB,
        split_axis=0,
        concat_axis=0,
        tiled=True,
    )
    got_flux = lax.all_to_all(
        flux_box.reshape(chan_local, slab_count, send_slots, comp_slots),
        SLAB,
        split_axis=1,
        concat_axis=1,
        tiled=True,
    )
    targets = got_pixels.reshape(-1)
    amounts = got_flux.reshape(chan_local, -1)
    raster = jnp.zeros((chan_local, slab_area), jnp.float32).at[:, targets].add(amounts)
    row_spectra = forward_rows(raster[0].reshape(rows_dev, row_width), length)
    columns = core_and_chips(row_spectra, (("slab_0", "slab_1"), "slab_2"), (1, 0), 2, 1)
    spectrum = forward_cols(columns, length)
    filtered = twiddle(spectrum, (psf_real[0], psf_imag[0]))
    narrowed = inverse_cols(filtered, length)
    returned = lax.all_to_all(narrowed, SLAB, split_axis=1, concat_axis=2, tiled=True)
    smeared = inverse_rows(returned, length)
    convolved = [dirty[0] - smeared]
    residual = jnp.stack(convolved)
    squares = jnp.sum(residual * residual, axis=(1, 2))
    peaks = jnp.max(jnp.abs(residual), axis=(1, 2))
    pixel_total = rows_dev * slab_count * row_width
    totals = taken_together(squares, SLAB)
    highest = over_copies(peaks, SLAB)
    rms_values, peak_values = rows_first((jnp.sqrt(totals / pixel_total), highest), "chan", (0, 0))
    return (residual, rms_values, peak_values)


def solution(mesh):
    torus = Mesh(
        mesh.devices.reshape(mesh.shape["chan"], 4, 8, 2), ("chan", "slab_0", "slab_1", "slab_2")
    )
    in_specs = (
        P("chan", SLAB, None),
        P(SLAB, None),
        P(SLAB),
        P(SLAB, None),
        P(SLAB),
        P("chan", SLAB, None),
        P("chan", None, SLAB),
        P("chan", None, SLAB),
    )
    out_specs = (P("chan", SLAB, None), P(), P())
    return jax.shard_map(
        on_device, mesh=torus, in_specs=in_specs, out_specs=out_specs, check_vma=False
    )
```

profile of v0, /device:TPU:1, one launch (start us, length us, event | category | flops | bytes accessed | tf_op | source)
XLA Modules:
  0.0 536.7 jit_solution(17369215564055994624)
XLA Ops:
  5.3 13.0 %all-to-all-start = ((s32[64,2,128]{2,1,0:T(2,128)}), s32[64,2,128]{2,1,0:T(2,128)S(1)}, u32[]{:S(2)}, u32[]{:S(2)}) async-start(s32[64,2,128]{2,1,0:T(2,128)} %bitcast.27), calls=%async_computation | async-start | bytes 131072 | tf_op jit(solution)/shard_map/all_to_all | solution.py:187
  20.5 7.6 %all-to-all-done = s32[64,2,128]{2,1,0:T(2,128)S(1)} async-done(((s32[64,2,128]{2,1,0:T(2,128)}), s32[64,2,128]{2,1,0:T(2,128)S(1)}, u32[]{:S(2)}, u32[]{:S(2)}) %all-to-all-start) | async-done | bytes 65568 | tf_op jit(solution)/shard_map/all_to_all | solution.py:187
  28.0 4.4 all-to-all-start.1
  32.5 9.8 %all-to-all-done.1 = f32[1,64,2,128]{3,2,0,1:T(2,128)S(1)} async-done(((f32[1,64,2,128]{3,2,0,1:T(2,128)}), f32[1,64,2,128]{3,2,0,1:T(2,128)S(1)}, u32[]{:S(2)}, u32[]{:S(2)}) %all-to-all-start.1) | async-done | bytes 65568 | tf_op jit(solution)/shard_map/all_to_all | solution.py:194
  42.3 102.5 %scatter_custom_fusion.2 = f32[262144]{0:T(1024)S(1)} fusion(s32[16384]{0:T(1024)S(1)} %bitcast.186, f32[16384]{0:T(1024)S(1)} %bitcast.185, f32[]{:T(128)} %constant.153.clone.1), kind=kCustom, calls=%fused_computation.52 | custom fusion | flops 16384 | bytes 1048580 | tf_op jit(solution)/shard_map/scatter-add | solution.py:203
  154.0 7.5 %all_to_all.47 = f32[32,2,2,64,128]{4,0,3,2,1:T(8,128)S(1)} all-to-all(f32[32,2,2,64,128]{4,0,3,2,1:T(8,128)S(1)} %copy.90), channel_id=1, replica_groups=mesh['chan'=4,'slab_0'=4,'slab_1'=8,'slab_2'=2] {'slab_2'}, dimensions={1} | all-to-all | bytes 8388608 | tf_op jit(solution)/shard_map/all_to_all | solution.py:32
  161.5 5.2 copy.91
  166.7 4.9 all-to-all-start.3
  172.7 91.4 %all-to-all-done.3 = f32[32,2,2,64,128]{4,1,3,2,0:T(2,128)} async-done(((f32[32,2,2,64,128]{4,1,3,2,0:T(2,128)}), f32[32,2,2,64,128]{4,1,3,2,0:T(2,128)}, u32[]{:S(2)}, u32[]{:S(2)}) %all-to-all-start.3) | async-done | bytes 4194336 | tf_op jit(solution)/shard_map/all_to_all | solution.py:32
  264.1 4.6 copy.92
  268.7 7.2 %convolution_bitcast_fusion = f32[2,128,64,128]{3,1,2,0:T(8,128)S(1)} fusion(f32[2,64,64,128,1]{3,1,0,2,4:T(8,128)S(1)} %bitcast.177, f32[1,64,2,128]{3,1,2,0:T(8,128)S(1)} %get-tuple-element.21, f32[1,64,2,128]{3,1,2,0:T(8,128)S(1)} %get-tuple-element.20), kind=kOutput, calls=%fused_computation.39 | convolution fusion | flops 3221258240 | bytes 12713984 | tf_op jit(solution)/shard_map/sabc,satk->tkbc/dot_general | solution.py:93
  280.1 12.5 %fusion.20 = f32[2,64,128,128]{3,1,2,0:T(8,128)S(1)} fusion(f32[2,128,64,128]{3,1,2,0:T(8,128)S(1)} %pad_maximum_fusion, f32[1,64,2,64]{1,3,0,2:T(8,128)S(1)} %get-tuple-element.23, f32[1,64,2,64]{1,3,0,2:T(8,128)S(1)} %get-tuple-element.22), kind=kOutput, calls=%fused_computation.37 | convolution fusion | flops 3221241856 | bytes 16842752 | tf_op jit(solution)/shard_map/skbc,sbtj->tjkc/dot_general | solution.py:93
  301.1 8.8 %fusion.15 = (f32[1,8192,128]{2,1,0:T(8,128)}, f32[1,8192,128]{2,1,0:T(8,128)}) fusion(f32[1,8192,128]{2,1,0:T(8,128)} %param.15, f32[1,64,128,128]{3,2,1,0:T(8,128)} %copy.96, f32[1,8192,128]{2,1,0:T(8,128)} %param.14, f32[1,64,128,128]{3,2,1,0:T(8,128)S(1)} %copy.95), kind=kLoop, calls=%fused_computation.25 | loop fusion | flops 6291456 | bytes 25165824 | tf_op jit(solution)/shard_map/sub | solution.py:101
  309.9 4.8 copy.97
  317.3 7.7 %fusion.23 = f32[2,128,64,128]{3,1,2,0:T(8,128)S(1)} fusion(f32[1,128,64,128]{3,1,0,2:T(8,128)S(1)} %copy.98, f32[1,128,64,128]{3,1,0,2:T(8,128)S(1)} %copy.97, f32[1,128,2,128]{1,3,0,2:T(8,128)S(1)} %get-tuple-element.19, f32[1,128,2,128]{1,3,0,2:T(8,128)S(1)} %get-tuple-element.18), kind=kOutput, calls=%fused_computation.38 | convolution fusion | flops 6444613632 | bytes 17039360 | tf_op jit(solution)/shard_map/sabc,sate->tebc/dot_general | solution.py:93
  329.3 9.4 %bitcast_multiply_fusion = f32[2,32,128,128]{3,1,2,0:T(8,128)S(1)} fusion(f32[2,128,64,128]{3,1,2,0:T(8,128)S(1)} %pad_maximum_fusion.1, f32[1,64,2,32]{1,3,0,2:T(8,128)S(1)} %get-tuple-element.25, f32[1,64,2,32]{1,3,0,2:T(8,128)S(1)} %get-tuple-element.24), kind=kOutput, calls=%fused_computation.22 | convolution fusion | flops 1611669504 | bytes 12615680 | tf_op jit(solution)/shard_map/sebc,sbtd->tdec/dot_general | solution.py:93
  341.2 15.6 %copy.101 = f32[2,4096,128]{2,0,1:T(2,128)S(1)} copy(f32[2,4096,128]{2,1,0:T(8,128)S(1)} %bitcast.180) | data formatting | bytes 8388608 | tf_op jit(solution)/shard_map/mul | solution.py:142
  356.9 106.6 %all_to_all.48 = f32[2,4096,128]{2,0,1:T(2,128)S(1)} all-to-all(f32[2,4096,128]{2,0,1:T(2,128)S(1)} %copy.101), channel_id=1, replica_groups=mesh['chan'=4,'slab_0'=4,'slab_1'=8,'slab_2'=2] {'slab_0','slab_1','slab..., dimensions={1} | all-to-all | bytes 8388608 | tf_op jit(solution)/shard_map/all_to_all | solution.py:209
  467.9 7.0 %reshape.554 = f32[2,64,128,64]{3,2,1,0:T(8,128)} reshape(f32[2,64,64,128]{3,2,1,0:T(8,128)} %bitcast.178) | data formatting | bytes 8388608 | tf_op jit(solution)/shard_map/reshape | solution.py:148
  474.9 15.6 %fusion.26 = f32[2,64,128,64]{2,3,1,0:T(8,128)S(1)} fusion(f32[2,64,128,64]{3,2,1,0:T(8,128)} %reshape.554, f32[1,128,2,128]{1,3,0,2:T(8,128)S(1)} %get-tuple-element.19, f32[1,128,2,128]{1,3,0,2:T(8,128)S(1)} %get-tuple-element.18), kind=kOutput, calls=%fused_computation.41 | convolution fusion | flops 3221291008 | bytes 8650752 | tf_op jit(solution)/shard_map/srab,sate->treb/dot_general | solution.py:93
  496.3 14.9 %all_to_all.49 = f32[64,1,1]{2,1,0:T(1,128)S(1)} all-to-all(f32[64,1,1]{2,1,0:T(1,128)S(1)} %broadcast_in_dim.15), channel_id=1, replica_groups=mesh['chan'=4,'slab_0'=4,'slab_1'=8,'slab_2'=2] {'slab_0','slab_1','slab..., dimensions={0} | all-to-all | bytes 512 | tf_op jit(solution)/shard_map/all_to_all | solution.py:44
  512.4 4.7 all-to-all-start.6
  518.5 8.1 %all-to-all-done.6 = f32[64,1,1]{2,1,0:T(1,128)S(1)} async-done(((f32[64,1,1]{2,1,0:T(1,128)}), f32[64,1,1]{2,1,0:T(1,128)S(1)}, u32[]{:S(2)}, u32[]{:S(2)}) %all-to-all-start.6) | async-done | bytes 288 | tf_op jit(solution)/shard_map/all_to_all | solution.py:44
  527.9 8.0 %all-gather = f32[4,1,2]{2,1,0:T(1,128)S(1)} all-gather(f32[1,1,2]{2,1,0:T(1,128)S(1)} %maximum_bitcast_fusion.15), channel_id=1, replica_groups=mesh['chan'=4,'slab_0'=4,'slab_1'=8,'slab_2'=2] {'chan'}, dimensions={0}, use_global_device_ids=true | all-gather | bytes 40 | tf_op jit(solution)/shard_map/all_gather | solution.py:61
  (52 shorter events, 53.4 us)
Async XLA Ops:
  5.3 22.8 %all-to-all-start = ((s32[64,2,128]{2,1,0:T(2,128)}), s32[64,2,128]{2,1,0:T(2,128)S(1)}, u32[]{:S(2)}, u32[]{:S(2)}) async-start(s32[64,2,128]{2,1,0:T(2,128)} %bitcast.27), calls=%async_computation | async-start | bytes 131072 | tf_op jit(solution)/shard_map/all_to_all | solution.py:187
  28.0 14.3 %all-to-all-start.1 = ((f32[1,64,2,128]{3,2,0,1:T(2,128)}), f32[1,64,2,128]{3,2,0,1:T(2,128)S(1)}, u32[]{:S(2)}, u32[]{:S(2)}) async-start(f32[1,64,2,128]{3,2,0,1:T(2,128)} %bitcast.31), calls=%async_computation.1 | async-start | bytes 131072 | tf_op jit(solution)/shard_map/all_to_all | solution.py:194
  166.7 97.4 %all-to-all-start.3 = ((f32[32,2,2,64,128]{4,1,3,2,0:T(2,128)}), f32[32,2,2,64,128]{4,1,3,2,0:T(2,128)}, u32[]{:S(2)}, u32[]{:S(2)}) async-start(f32[32,2,2,64,128]{4,1,3,2,0:T(2,128)} %copy.91), calls=%async_computation.3 | async-start | bytes 8388608 | tf_op jit(solution)/shard_map/all_to_all | solution.py:32
  309.9 4.8 copy-start
  491.4 2.4 copy-start.1
  512.4 14.1 %all-to-all-start.6 = ((f32[64,1,1]{2,1,0:T(1,128)}), f32[64,1,1]{2,1,0:T(1,128)S(1)}, u32[]{:S(2)}, u32[]{:S(2)}) async-start(f32[64,1,1]{2,1,0:T(1,128)} %broadcast_in_dim.16), calls=%async_computation.6 | async-start | bytes 65536 | tf_op jit(solution)/shard_map/all_to_all | solution.py:44
where the time goes:
time: 541 us; the launch traced here: 537 us
  blocking collectives  137 us (25%)
  other arithmetic  134 us (25%)
  waiting for transfers between devices  117 us (22%)
  matrix products  61.8 us (11%)
  local copies, waits for them, and re-layouts  58.7 us (11%)
  starting transfers between devices  26.9 us (5%)
    all_to_all x1, blocking collectives, on_device(): lax.all_to_all(narrowed, SLAB, split_axis=1, concat_axis=2, tiled=True)  107 us
    scatter-add x1, other arithmetic, on_device(): jnp.zeros((chan_local, slab_area), jnp.float32).at[:, targets].add(amounts)  102 us
    all_to_all x1, waiting for transfers between devices, turned_blocks(): lax.all_to_all(pieces, axes[k], split_axis=k, concat_axis=k, tiled=True)  91.4 us
    dot_general x8, matrix products, contract(): return jnp.einsum(pattern, first_op, second_op, precision=PRECISE)  61.8 us
    mul x2, local copies, waits for them, and re-layouts, inverse_cols(): return result.reshape(2, length // 2, col_count) * (1.0 / length)  18.1 us
    sub x5, other arithmetic, twiddle(): value_re * phase_re - value_im * phase_im  17.1 us
    all_to_all x1, blocking collectives, sent_to_all(): return lax.all_to_all(copies, axis, split_axis=0, concat_axis=0, tiled=True)  14.9 us
    all_to_all x1, starting transfers between devices, on_device(): lax.all_to_all(pixel_box.reshape(slab_count, send_slots, comp_slots), SLA...  13 us
  transfers between devices with their start and end apart: 4, of which 4 were waited for; matrix products, arithmetic and copies ran while one was open for 1% of the time, Pallas kernels for 0%

commit v1 on v0

v1 whole, which is shorter than its diff:
```python
import functools
import math

import jax
import jax.numpy as jnp
import numpy as np
from jax import lax
from jax.experimental import pallas as pl
from jax.experimental.pallas import tpu as pltpu
from jax.sharding import Mesh
from jax.sharding import PartitionSpec as P

TILE_R = 64
TILE_C = 128
SLAB = ("slab_0", "slab_1", "slab_2")
ROWS = 64
COLS = 128
PEERS = 64
LENGTH = 8192
TILES = 32

BF = jnp.bfloat16
F32 = jnp.float32


def halves(table):
    table = np.asarray(table, np.float32)
    high = table.astype(jnp.bfloat16)
    low = (table - high.astype(np.float32)).astype(jnp.bfloat16)
    return high, low


def turns(first, second, length):
    return 2.0 * math.pi * (np.outer(first, second) % length) / length


def row_tables():
    j, tc, cc, d = np.arange(COLS), np.arange(TILES), np.arange(TILE_C), np.arange(PEERS)
    angle = turns(j, tc, 64)
    high, low = halves(np.concatenate([np.cos(angle), -np.sin(angle)], axis=0))
    first = np.concatenate([high, high, low], axis=1)
    angle = turns(j, cc, LENGTH)
    tw_re, tw_im = np.cos(angle).astype(np.float32), (-np.sin(angle)).astype(np.float32)
    angle = turns(d, cc, 64)
    block = np.stack(
        [
            np.concatenate([np.cos(angle), np.sin(angle)], axis=1),
            np.concatenate([-np.sin(angle), np.cos(angle)], axis=1),
        ],
        axis=1,
    ).reshape(2 * PEERS, 2 * TILE_C)
    high, low = halves(block)
    second = np.concatenate([high, low], axis=0)
    return first, tw_re, tw_im, second


def column_tables():
    a, k, m, b = np.arange(64), np.arange(128), np.arange(64), np.arange(64)
    angle = turns(k, a, 128)
    c, s = np.cos(angle), np.sin(angle)
    first = np.stack([np.stack([c, s], axis=2), np.stack([-s, c], axis=2)], axis=1)
    first_hi, first_lo = halves(first.reshape(256, 128))
    angle = turns(m, b, 64)
    c, s = np.cos(angle), np.sin(angle)
    second = np.block([[c, s], [-s, c]]).astype(np.float32)
    second_turn = np.block([[-s, c], [-c, -s]]).astype(np.float32)
    angle = turns(k, b, LENGTH)
    phase = np.stack([np.tile(np.cos(angle), (1, 2)), np.tile(np.sin(angle), (1, 2))], axis=1)
    angle = turns(b, m, 64)
    c, s = np.cos(angle), np.sin(angle)
    third_hi, third_lo = halves(np.block([[c, -s], [s, c]]))
    third = np.concatenate([third_hi, third_lo], axis=1)
    angle = turns(a, k, 128)
    c, s = np.cos(angle) * 2.0**-26, np.sin(angle) * 2.0**-26
    fourth = np.stack([np.stack([c, -s], axis=2), np.stack([s, c], axis=2)], axis=1)
    fourth_turn = np.stack([np.stack([-s, -c], axis=2), np.stack([c, -s], axis=2)], axis=1)
    angle = np.repeat(turns(b, k, LENGTH), 2, axis=1)
    last_phase = np.stack([np.cos(angle), np.sin(angle)], axis=1)
    return (
        np.concatenate([first_hi, first_hi], axis=1),
        first_lo,
        second,
        second_turn,
        phase.astype(np.float32),
        third,
        fourth.reshape(128, 256).astype(np.float32),
        fourth_turn.reshape(128, 256).astype(np.float32),
        last_phase.astype(np.float32),
    )


def inverse_tables():
    d, q, j, n2, n1 = np.arange(64), np.arange(64), np.arange(128), np.arange(128), np.arange(32)
    angle = turns(q, d, 64)
    c, s = np.cos(angle), np.sin(angle)
    first = np.concatenate(
        [
            np.stack([c, -s], axis=2).reshape(64, 128),
            np.stack([s, c], axis=2).reshape(64, 128),
        ],
        axis=0,
    )
    first_hi, first_lo = halves(first)
    angle = turns(n2, j, LENGTH)
    tw_re, tw_im = np.cos(angle).astype(np.float32), np.sin(angle).astype(np.float32)
    angle = turns(n1, j, 64)
    high, low = halves(np.concatenate([np.cos(angle), -np.sin(angle)], axis=1))
    return (
        np.concatenate([first_hi, first_hi], axis=1),
        first_lo,
        tw_re,
        tw_im,
        np.concatenate([high, low], axis=0),
    )


def split(value):
    high = value.astype(BF)
    low = (value - high.astype(F32)).astype(BF)
    return high, low


def mm(first, second):
    return jnp.dot(first, second, preferred_element_type=F32)


def mm_nt(first, second):
    return lax.dot_general(
        first, second, (((1,), (1,)), ((), ())), preferred_element_type=F32
    )


GROUP = 4


def rows_kernel(tile_ref, got_ref, first_ref, twr_ref, twi_ref, second_ref, out_ref, image):
    step = pl.program_id(0)
    blocks = got_ref.shape[0] // 2

    @pl.when(step == 0)
    def _():
        image[...] = jnp.zeros_like(image)
        row_ids = lax.broadcasted_iota(jnp.int32, (TILE_R, 128), 0)
        col_ids = lax.broadcasted_iota(jnp.int32, (TILE_C, 128), 0)

        def body(it, carry):
            tiles = []
            both = got_ref[pl.ds(pl.multiple_of(it * 2 * GROUP, 2 * GROUP), 2 * GROUP), :]
            for g in range(GROUP):
                place = both[2 * g : 2 * g + 1].astype(jnp.int32)
                flux = both[2 * g + 1 : 2 * g + 2]
                row = (place >> 7) & (TILE_R - 1)
                col = place & (TILE_C - 1)
                high = flux.astype(BF).astype(F32)
                low = flux - high
                here = row_ids == row
                lhs = jnp.concatenate(
                    [jnp.where(here, high, 0.0), jnp.where(here, low, 0.0)], axis=0
                ).astype(BF)
                rhs = jnp.where(col_ids == col, 1.0, 0.0).astype(BF)
                both_parts = mm_nt(lhs, rhs)
                tiles.append(both_parts[:TILE_R] + both_parts[TILE_R:])
            for g in range(GROUP):
                at = pl.ds(pl.multiple_of(tile_ref[it * GROUP + g] * TILE_R, TILE_R), TILE_R)
                image[at, :] += tiles[g]
            return carry

        lax.fori_loop(0, blocks // GROUP, body, 0)

    rows = out_ref.shape[1]
    out = out_ref.reshape(2 * PEERS * rows, COLS)
    for pair in range(rows // 2):
        parts = []
        for e in range(2):
            x = image[pl.ds(step * rows + 2 * pair + e, TILES, stride=TILE_R), :]
            high, low = split(x)
            parts.append(jnp.concatenate([high, low, high], axis=0))
        partial = mm(first_ref[...], jnp.concatenate(parts, axis=1))
        turned = []
        for e in range(2):
            re = partial[:COLS, e * TILE_C : (e + 1) * TILE_C]
            im = partial[COLS:, e * TILE_C : (e + 1) * TILE_C]
            turned.append(
                jnp.concatenate(
                    [
                        re * twr_ref[...] - im * twi_ref[...],
                        re * twi_ref[...] + im * twr_ref[...],
                    ],
                    axis=1,
                )
            )
        high, low = split(jnp.concatenate(turned, axis=0))
        full = mm_nt(second_ref[...], high)
        part = mm_nt(second_ref[: 2 * PEERS], low)
        result = full[: 2 * PEERS] + full[2 * PEERS :] + part
        for e in range(2):
            out[pl.ds(2 * pair + e, 2 * PEERS, stride=rows), :] = result[
                :, e * COLS : (e + 1) * COLS
            ]


def whole(shape):
    return pl.BlockSpec(shape, lambda *_: (0,) * len(shape))


def forward_rows(tiles, got, rows=8):
    first, twr, twi, second = row_tables()
    return pl.pallas_call(
        rows_kernel,
        out_shape=jax.ShapeDtypeStruct((2 * PEERS, ROWS, COLS), F32),
        grid=(ROWS // rows,),
        in_specs=[
            pl.BlockSpec(memory_space=pltpu.SMEM),
            whole(got.shape),
            whole(first.shape),
            whole(twr.shape),
            whole(twi.shape),
            whole(second.shape),
        ],
        out_specs=pl.BlockSpec((2 * PEERS, rows, COLS), lambda i: (0, i, 0)),
        scratch_shapes=[pltpu.VMEM((TILES * TILE_R, TILE_C), F32)],
        name="rows",
    )(tiles, got, jnp.asarray(first), jnp.asarray(twr), jnp.asarray(twi), jnp.asarray(second))


STEPS = 8


def columns_kernel(
    x_ref,
    pr_ref,
    pi_ref,
    first_ref,
    first_lo_ref,
    second_ref,
    second_turn_ref,
    phase_ref,
    third_ref,
    fourth_ref,
    fourth_turn_ref,
    last_phase_ref,
    out_ref,
    held,
):
    step = pl.program_id(0)
    rows = x_ref.shape[1]
    per = pr_ref.shape[1]

    @pl.when(step < STEPS)
    def _():
        x = x_ref.reshape(128 * rows, COLS)
        for pair in range(rows // 2):
            values = jnp.concatenate(
                [x[pl.ds(2 * pair + e, 128, stride=rows), :] for e in range(2)], axis=1
            )
            high, low = split(values)
            both = jnp.concatenate([high, low], axis=0)
            result = mm(first_ref[...], both) + mm(first_lo_ref[...], high)
            for e in range(2):
                at = pl.multiple_of((step * rows + 2 * pair + e) * 256, 256)
                held[pl.ds(at, 256), :] = result[:, e * COLS : (e + 1) * COLS]

    @pl.when(jnp.logical_and(step >= STEPS, step < 2 * STEPS))
    def _():
        pr = pr_ref.reshape(64 * per, COLS)
        pi = pi_ref.reshape(64 * per, COLS)

        def body(i, carry):
            k = (step - STEPS) * per + i
            table = (
                second_ref[...] * phase_ref[k, 0:1, :] + second_turn_ref[...] * phase_ref[k, 1:2, :]
            )
            table_hi, table_lo = split(table)
            values = jnp.concatenate(
                [held[pl.ds(2 * k + s, 64, stride=256), :] for s in range(2)], axis=0
            )
            high, low = split(values)
            spectrum = mm(
                jnp.concatenate([table_hi, table_lo], axis=1),
                jnp.concatenate([high, high], axis=0),
            ) + mm(table_hi, low)
            re, im = spectrum[:64], spectrum[64:]
            psf_re = pr[pl.ds(i, 64, stride=per), :]
            psf_im = pi[pl.ds(i, 64, stride=per), :]
            filtered = jnp.concatenate(
                [re * psf_re - im * psf_im, re * psf_im + im * psf_re], axis=0
            )
            high, low = split(filtered)
            third = third_ref[...]
            result = mm(third, jnp.concatenate([high, high], axis=0)) + mm(third[:, :128], low)
            for s in range(2):
                held[pl.ds(2 * k + s, 64, stride=256), :] = result[64 * s : 64 * s + 64]
            return carry

        lax.fori_loop(0, per, body, 0, unroll=4)

    @pl.when(step >= 2 * STEPS)
    def _():
        out = out_ref.reshape(128 * rows, COLS)
        for pair in range(rows // 2):
            for e in range(2):
                row = (step - 2 * STEPS) * rows + 2 * pair + e
                table = (
                    fourth_ref[...] * last_phase_ref[row, 0:1, :]
                    + fourth_turn_ref[...] * last_phase_ref[row, 1:2, :]
                )
                table_hi, table_lo = split(table)
                at = pl.multiple_of(row * 256, 256)
                high, low = split(held[pl.ds(at, 256), :])
                full = mm(jnp.concatenate([table_hi, table_lo], axis=0), high)
                result = full[:128] + full[128:] + mm(table_hi, low)
                out[pl.ds(2 * pair + e, 128, stride=rows), :] = result


def columns(values, psf_re, psf_im):
    tables = column_tables()
    rows = ROWS // STEPS
    per = 128 // STEPS
    psf_re = psf_re.reshape(64, 128, COLS)
    psf_im = psf_im.reshape(64, 128, COLS)

    def psf_at(i):
        return (0, jnp.clip(i - STEPS, 0, STEPS - 1), 0)

    return pl.pallas_call(
        columns_kernel,
        out_shape=jax.ShapeDtypeStruct((128, ROWS, COLS), F32),
        grid=(3 * STEPS,),
        in_specs=[
            pl.BlockSpec((128, rows, COLS), lambda i: (0, jnp.minimum(i, STEPS - 1), 0)),
            pl.BlockSpec((64, per, COLS), psf_at),
            pl.BlockSpec((64, per, COLS), psf_at),
        ]
        + [whole(t.shape) for t in tables],
        out_specs=pl.BlockSpec(
            (128, rows, COLS), lambda i: (0, jnp.maximum(i - 2 * STEPS, 0), 0)
        ),
        scratch_shapes=[pltpu.VMEM((64 * 256, COLS), F32)],
        name="columns",
    )(values, psf_re, psf_im, *[jnp.asarray(t) for t in tables])


def inverse_kernel(
    y_ref, dirty_ref, first_ref, first_lo_ref, twr_ref, twi_ref, last_ref, out_ref, stat_ref, smear
):
    step = pl.program_id(0)
    rows = y_ref.shape[1]
    y = y_ref.reshape(128 * rows, COLS)
    for pair in range(rows // 2):
        values = jnp.concatenate(
            [y[pl.ds(2 * pair + e, 128, stride=rows), :] for e in range(2)], axis=1
        )
        high, low = split(values)
        partial = mm(first_ref[...], jnp.concatenate([high, low], axis=0)) + mm(
            first_lo_ref[...], high
        )
        turned = []
        for e in range(2):
            re = partial[:64, e * COLS : (e + 1) * COLS]
            im = partial[64:, e * COLS : (e + 1) * COLS]
            re = jnp.concatenate([re, re], axis=0)
            im = jnp.concatenate([im, im], axis=0)
            turned.append(
                jnp.concatenate(
                    [
                        re * twr_ref[...] - im * twi_ref[...],
                        re * twi_ref[...] + im * twr_ref[...],
                    ],
                    axis=1,
                )
            )
        high, low = split(jnp.concatenate(turned, axis=0))
        full = mm_nt(last_ref[...], high)
        result = full[:TILES] + full[TILES:] + mm_nt(last_ref[:TILES], low)
        for e in range(2):
            smear[pl.ds(2 * pair + e, TILES, stride=rows), :] = result[
                :, e * TILE_C : (e + 1) * TILE_C
            ]
    squares = jnp.zeros((rows, TILE_C), F32)
    peaks = jnp.zeros((rows, TILE_C), F32)
    for t in range(TILES):
        lanes = slice(t * TILE_C, (t + 1) * TILE_C)
        rest = dirty_ref[:, lanes] - smear[t * rows : (t + 1) * rows, :]
        out_ref[:, lanes] = rest
        squares += rest * rest
        peaks = jnp.maximum(peaks, jnp.abs(rest))

    @pl.when(step == 0)
    def _():
        stat_ref[...] = jnp.zeros_like(stat_ref)

    stat_ref[0:8, :] += squares
    stat_ref[8:16, :] = jnp.maximum(stat_ref[8:16, :], peaks)


def inverse_rows(values, dirty):
    tables = inverse_tables()
    rows = 8
    width = dirty.shape[1]
    return pl.pallas_call(
        inverse_kernel,
        out_shape=(
            jax.ShapeDtypeStruct((ROWS, width), F32),
            jax.ShapeDtypeStruct((16, TILE_C), F32),
        ),
        grid=(ROWS // rows,),
        in_specs=[
            pl.BlockSpec((128, rows, COLS), lambda i: (0, i, 0)),
            pl.BlockSpec((rows, width), lambda i: (i, 0)),
        ]
        + [whole(t.shape) for t in tables],
        out_specs=(
            pl.BlockSpec((rows, width), lambda i: (i, 0)),
            pl.BlockSpec((16, TILE_C), lambda i: (0, 0)),
        ),
        scratch_shapes=[pltpu.VMEM((TILES * rows, TILE_C), F32)],
        name="inverse",
    )(values, dirty, *[jnp.asarray(t) for t in tables])


def boxes(flux, offsets, counts, dest_owner, dest_tile):
    blocks, slots = offsets.shape
    live = jnp.arange(slots, dtype=jnp.int32)[None, :] < counts[:, None]
    weights = jnp.where(live, flux, 0.0)
    places = (dest_tile[:, None] * (TILE_R * TILE_C) + offsets).astype(F32)
    payload = jnp.concatenate([places, weights], axis=1)
    owner = dest_owner[:, 0]
    ids = jnp.arange(blocks, dtype=jnp.int32)
    same = (owner[:, None] == owner[None, :]) & (ids[None, :] < ids[:, None])
    rank = jnp.sum(same.astype(jnp.int32), axis=1)
    slot = owner * 2 + rank
    marks = (slot[None, :] == jnp.arange(2 * PEERS, dtype=jnp.int32)[:, None]).astype(F32)
    box = jnp.dot(marks, payload, precision=lax.Precision.HIGHEST)
    return box.reshape(PEERS, 4, slots)


def on_device(flux, offsets, counts, dest_owner, dest_tile, dirty, psf_real, psf_imag):
    box = boxes(flux[0], offsets, counts, dest_owner, dest_tile)
    got = lax.all_to_all(box, SLAB, split_axis=0, concat_axis=0, tiled=True)
    tiles = got.reshape(2 * PEERS, 2, -1)[:, 0, 0].astype(jnp.int32) // (TILE_R * TILE_C)
    rows = forward_rows(tiles, got.reshape(4 * PEERS, -1))
    rows = rows.reshape(PEERS, 2, ROWS, COLS)
    turned = lax.all_to_all(rows, SLAB, split_axis=0, concat_axis=0, tiled=True)
    back = columns(turned.reshape(2 * PEERS, ROWS, COLS), psf_real[0], psf_imag[0])
    back = back.reshape(PEERS, 2, ROWS, COLS)
    home = lax.all_to_all(back, SLAB, split_axis=0, concat_axis=0, tiled=True)
    residual, stats = inverse_rows(home.reshape(2 * PEERS, ROWS, COLS), dirty[0])
    own = jnp.stack([jnp.sum(stats[:8]), jnp.max(stats[8:])])
    every = lax.all_gather(own[None], ("chan",) + SLAB, axis=0, tiled=True)
    every = every.reshape(-1, PEERS, 2)
    pixel_total = PEERS * dirty.shape[1] * dirty.shape[2]
    rms_values = jnp.sqrt(jnp.sum(every[:, :, 0], axis=1) / pixel_total)
    peak_values = jnp.max(every[:, :, 1], axis=1)
    return residual[None], rms_values, peak_values


def solution(mesh):
    torus = Mesh(
        mesh.devices.reshape(mesh.shape["chan"], 4, 8, 2), ("chan", "slab_0", "slab_1", "slab_2")
    )
    in_specs = (
        P("chan", SLAB, None),
        P(SLAB, None),
        P(SLAB),
        P(SLAB, None),
        P(SLAB),
        P("chan", SLAB, None),
        P("chan", None, SLAB),
        P("chan", None, SLAB),
    )
    out_specs = (P("chan", SLAB, None), P(), P())
    return jax.shard_map(
        on_device, mesh=torus, in_specs=in_specs, out_specs=out_specs, check_vma=False
    )
```

time: 541 us -> 381 us (0.70)
  other arithmetic: 134 us -> 10.8 us
  Pallas kernels: 0 us -> 66.2 us
  blocking collectives: 137 us -> 201 us
  matrix products: 61.8 us -> 0.2 us
  local copies, waits for them, and re-layouts: 58.7 us -> 0.21 us
  waiting for transfers between devices: 117 us -> 95.8 us
  starting transfers between devices: 26.9 us -> 6.03 us
    scatter-add x1 -> x0, other arithmetic: 102 us -> none  [on_device(): jnp.zeros((chan_local, slab_area), jnp.float32).at[:, targets].add(amounts)]
    unnamed x0 -> x1, blocking collectives: none -> 76 us
    pallas_call x0 -> x3, Pallas kernels: none -> 66.2 us  [the longest x1 39.4 us: columns(): pl.pallas_call(columns_kernel, out_shape=jax.ShapeDtypeStruct((128, ROWS,...]
    dot_general x8 -> x1, matrix products: 61.8 us -> 0.2 us  [boxes(): box = jnp.dot(marks, payload, precision=lax.Precision.HIGHEST)]
    all_to_all x4 -> x1, waiting for transfers between devices: 117 us -> 95.8 us  [on_device(): home = lax.all_to_all(back, SLAB, split_axis=0, concat_axis=0, tiled=True)]
    all_to_all x4 -> x1, starting transfers between devices: 26.9 us -> 6.03 us  [on_device(): home = lax.all_to_all(back, SLAB, split_axis=0, concat_axis=0, tiled=True)]
    mul x3 -> x0, local copies, waits for them, and re-layouts: 18.3 us -> none  [the longest x2 18.1 us: inverse_cols(): return result.reshape(2, length // 2, col_count) * (1.0 / length)]
    sub x5 -> x0, other arithmetic: 17.1 us -> none  [twiddle(): value_re * phase_re - value_im * phase_im]
  transfers between devices with their start and end apart: 4 -> 1, of which waited for: 4 -> 1; matrix products, arithmetic and copies ran while one was open for 1% -> 0% of each run, Pallas kernels for 0% -> 0%
where the time goes in v1:
time: 381 us
  blocking collectives  201 us (53%)
  waiting for transfers between devices  95.8 us (25%)
  Pallas kernels  66.2 us (17%)
  other arithmetic  10.8 us (3%)
  starting transfers between devices  6.03 us (2%)
    all_to_all x1, blocking collectives, on_device(): turned = lax.all_to_all(rows, SLAB, split_axis=0, concat_axis=0, tiled=True)  102 us
    all_to_all x1, waiting for transfers between devices, on_device(): home = lax.all_to_all(back, SLAB, split_axis=0, concat_axis=0, tiled=True)  95.8 us
    unnamed x1, blocking collectives  76 us
    pallas_call x1, Pallas kernels, columns(): pl.pallas_call(columns_kernel, out_shape=jax.ShapeDtypeStruct((128, ROWS,...  39.4 us
    all_to_all x1, blocking collectives, on_device(): got = lax.all_to_all(box, SLAB, split_axis=0, concat_axis=0, tiled=True)  23.1 us
    pallas_call x1, Pallas kernels, forward_rows(): pl.pallas_call(rows_kernel, out_shape=jax.ShapeDtypeStruct((2 * PEERS, RO...  16.9 us
    pallas_call x1, Pallas kernels, inverse_rows(): pl.pallas_call(inverse_kernel, out_shape=(jax.ShapeDtypeStruct((ROWS, wid...  9.85 us
  transfers between devices with their start and end apart: 1, of which 1 were waited for; matrix products, arithmetic and copies ran while one was open for 0% of the time, Pallas kernels for 0%

profile of v1, /device:TPU:1, one launch (start us, length us, event | category | flops | bytes accessed | tf_op | source)
XLA Modules:
  0.0 380.6 jit_solution(16226363482106095006)
XLA Ops:
  0.6 0.7 broadcast_multiply_fusion
  1.3 0.9 convert_reduce_fusion
  2.2 0.7 multiply_add_fusion
  2.9 0.8 add_convert_fusion
  3.7 0.8 bitcast_select_fusion
  4.5 0.2 fusion.1
  4.7 0.1 reshape.43
  4.8 23.1 %all_to_all.15 = f32[64,4,128]{2,1,0:T(4,128)S(1)} all-to-all(f32[64,4,128]{2,1,0:T(4,128)S(1)} %reshape.43), channel_id=1, replica_groups=mesh['chan'=4,'slab_0'=4,'slab_1'=8,'slab_2'=2] {'slab_0','slab_1','slab..., dimensions={0} | all-to-all | bytes 262144 | tf_op jit(solution)/shard_map/all_to_all | solution.py:439
  27.9 0.0 copy-start
  27.9 2.4 fusion
  30.3 0.5 and_select_fusion.tile_ref
  30.8 0.0 copy-done
  30.8 16.9 %rows.1 = f32[128,64,128]{2,1,0:T(8,128)} custom-call(s32[128]{0:T(128)} %and_select_fusion.tile_ref, f32[256,128]{1,0:T(8,128)} %bitcast.23, bf16[256,96]{1,0:T(8,128)(2,1)} %constant.62.clone.first_ref, f32[128,128]{1,0:T(8,128)} %constant.63.clone.twr_ref, f32[128,128]{1,0:T(8,128)} %constant.64.clone.twi_ref, bf16[256,256]{1,0:T(8,128)(2,1)} %constant.65.clone.second_ref), custom_call_target="tpu_custom_call" | custom-call | tf_op jit(solution)/shard_map/rows/pallas_call | solution.py:208
  47.7 101.6 %all_to_all.16 = f32[64,2,64,128]{3,2,1,0:T(8,128)} all-to-all(f32[64,2,64,128]{3,2,1,0:T(8,128)} %bitcast.16), channel_id=1, replica_groups=mesh['chan'=4,'slab_0'=4,'slab_1'=8,'slab_2'=2] {'slab_0','slab_1','slab..., dimensions={0} | all-to-all | bytes 8388608 | tf_op jit(solution)/shard_map/all_to_all | solution.py:443
  149.3 39.4 %columns.1 = f32[128,64,128]{2,1,0:T(8,128)} custom-call(f32[128,64,128]{2,1,0:T(8,128)} %bitcast.18, f32[64,128,128]{2,1,0:T(8,128)} %bitcast.19, f32[64,128,128]{2,1,0:T(8,128)} %bitcast.20, bf16[256,256]{1,0:T(8,128)(2,1)} %constant.66.clone.first_ref, bf16[256,128]{1,0:T(8,128)(2,1)} %constant.67.clone.first_lo_ref, ...), custom_call_target="tpu_custom_call" | custom-call | tf_op jit(solution)/shard_map/columns/pallas_call | solution.py:325
  188.8 6.0 %all-to-all-start.2 = ((f32[64,2,64,128]{3,2,1,0:T(8,128)}), f32[64,2,64,128]{3,2,1,0:T(8,128)}, u32[]{:S(2)}, u32[]{:S(2)}) async-start(f32[64,2,64,128]{3,2,1,0:T(8,128)} %bitcast.17), calls=%async_computation.2 | async-start | bytes 8388608 | tf_op jit(solution)/shard_map/all_to_all | solution.py:446
  194.8 95.8 %all-to-all-done.2 = f32[64,2,64,128]{3,2,1,0:T(8,128)} async-done(((f32[64,2,64,128]{3,2,1,0:T(8,128)}), f32[64,2,64,128]{3,2,1,0:T(8,128)}, u32[]{:S(2)}, u32[]{:S(2)}) %all-to-all-start.2) | async-done | bytes 4194336 | tf_op jit(solution)/shard_map/all_to_all | solution.py:446
  290.6 9.8 %inverse.1 = (f32[64,4096]{1,0:T(8,128)}, f32[16,128]{1,0:T(8,128)}) custom-call(f32[128,64,128]{2,1,0:T(8,128)} %bitcast.9.y_ref, f32[64,4096]{1,0:T(8,128)} %bitcast.21, bf16[128,256]{1,0:T(8,128)(2,1)} %constant.75.clone.first_ref, bf16[128,128]{1,0:T(8,128)(2,1)} %constant.76.clone.first_lo_ref, f32[128,128]{1,0:T(8,128)} %constant.63.clone.twr_ref, ...), custom_call_target="tpu_custom_call" | custom-call | tf_op jit(solution)/shard_map/inverse/pallas_call | solution.py:400
  300.5 1.3 slice_reduce_fusion.3
  301.8 1.5 maximum_dynamic-update-slice_fusion
  303.2 76.0 %all-reduce = f32[512]{0:T(512)S(1)} all-reduce(f32[512]{0:T(512)S(1)} %maximum_dynamic-update-slice_fusion), channel_id=2, replica_groups=mesh['chan'=4,'slab_0'=4,'slab_1'=8,'slab_2'=2] {'chan','slab_0','slab_1..., use_global_device_ids=true, to_apply=%add | all-reduce | flops 512 | bytes 4096
  379.2 0.1 reshape.50
  379.4 0.7 slice_reduce_fusion
  380.1 0.5 multiply_sqrt_fusion
  (1 shorter events, 0.0 us)
Async XLA Ops:
  27.9 2.9 copy-start
  188.8 101.9 %all-to-all-start.2 = ((f32[64,2,64,128]{3,2,1,0:T(8,128)}), f32[64,2,64,128]{3,2,1,0:T(8,128)}, u32[]{:S(2)}, u32[]{:S(2)}) async-start(f32[64,2,64,128]{3,2,1,0:T(8,128)} %bitcast.17), calls=%async_computation.2 | async-start | bytes 8388608 | tf_op jit(solution)/shard_map/all_to_all | solution.py:446

commit v2 on v1

--- a/solution.py
+++ b/solution.py
@@ -41,6 +41,7 @@
     first = np.concatenate([high, high, low], axis=1)
     angle = turns(j, cc, LENGTH)
     tw_re, tw_im = np.cos(angle).astype(np.float32), (-np.sin(angle)).astype(np.float32)
+    d = d.reshape(4, 8, 2)[:, np.arange(12) % 8].transpose(1, 0, 2).reshape(-1)
     angle = turns(d, cc, 64)
     block = np.stack(
         [
@@ -48,10 +49,8 @@
             np.concatenate([-np.sin(angle), np.cos(angle)], axis=1),
         ],
         axis=1,
-    ).reshape(2 * PEERS, 2 * TILE_C)
-    high, low = halves(block)
-    second = np.concatenate([high, low], axis=0)
-    return first, tw_re, tw_im, second
+    ).reshape(-1, 2 * TILE_C)
+    return first, tw_re, tw_im, *halves(block)
 
 
 def column_tables():
@@ -133,9 +132,13 @@
 GROUP = 4
 
 
-def rows_kernel(tile_ref, got_ref, first_ref, twr_ref, twi_ref, second_ref, out_ref, image):
+def rows_kernel(
+    tile_ref, got_ref, first_ref, twr_ref, twi_ref, high_ref, low_ref, own_ref, far_ref, image
+):
     step = pl.program_id(0)
     blocks = got_ref.shape[0] // 2
+    rows = own_ref.shape[1]
+    z = tile_ref[blocks]
 
     @pl.when(step == 0)
     def _():
@@ -167,36 +170,49 @@
 
         lax.fori_loop(0, blocks // GROUP, body, 0)
 
-    rows = out_ref.shape[1]
-    out = out_ref.reshape(2 * PEERS * rows, COLS)
-    for pair in range(rows // 2):
-        parts = []
-        for e in range(2):
-            x = image[pl.ds(step * rows + 2 * pair + e, TILES, stride=TILE_R), :]
-            high, low = split(x)
-            parts.append(jnp.concatenate([high, low, high], axis=0))
-        partial = mm(first_ref[...], jnp.concatenate(parts, axis=1))
-        turned = []
-        for e in range(2):
-            re = partial[:COLS, e * TILE_C : (e + 1) * TILE_C]
-            im = partial[COLS:, e * TILE_C : (e + 1) * TILE_C]
-            turned.append(
-                jnp.concatenate(
-                    [
-                        re * twr_ref[...] - im * twi_ref[...],
-                        re * twi_ref[...] + im * twr_ref[...],
-                    ],
-                    axis=1,
+    def chunk(base, reach, out_ref):
+        many = (2 * reach + 1) * 16
+        out = out_ref.reshape(many * rows, COLS)
+        at = pl.ds(pl.multiple_of(lax.rem(z + 8 - reach, 8) * 16, 16), many)
+        table_hi, table_lo = high_ref[at, :], low_ref[at, :]
+        table = jnp.concatenate([table_hi, table_lo], axis=0)
+        for pair in range(rows // 2):
+            parts = []
+            for e in range(2):
+                x = image[pl.ds(base + 2 * pair + e, TILES, stride=TILE_R), :]
+                high, low = split(x)
+                parts.append(jnp.concatenate([high, low, high], axis=0))
+            partial = mm(first_ref[...], jnp.concatenate(parts, axis=1))
+            turned = []
+            for e in range(2):
+                re = partial[:COLS, e * TILE_C : (e + 1) * TILE_C]
+                im = partial[COLS:, e * TILE_C : (e + 1) * TILE_C]
+                turned.append(
+                    jnp.concatenate(
+                        [
+                            re * twr_ref[...] - im * twi_ref[...],
+                            re * twi_ref[...] + im * twr_ref[...],
+                        ],
+                        axis=1,
+                    )
                 )
-            )
-        high, low = split(jnp.concatenate(turned, axis=0))
-        full = mm_nt(second_ref[...], high)
-        part = mm_nt(second_ref[: 2 * PEERS], low)
-        result = full[: 2 * PEERS] + full[2 * PEERS :] + part
-        for e in range(2):
-            out[pl.ds(2 * pair + e, 2 * PEERS, stride=rows), :] = result[
-                :, e * COLS : (e + 1) * COLS
-            ]
+            high, low = split(jnp.concatenate(turned, axis=0))
+            full = mm_nt(table, high)
+            result = full[:many] + full[many:] + mm_nt(table_hi, low)
+            for e in range(2):
+                out[pl.ds(2 * pair + e, many, stride=rows), :] = result[
+                    :, e * COLS : (e + 1) * COLS
+                ]
+
+    chunks = ROWS // rows
+
+    @pl.when(step < chunks)
+    def _():
+        chunk(step * rows, 2, own_ref)
+
+    @pl.when(step >= chunks)
+    def _():
+        chunk(TILES * TILE_R + (step - chunks) * rows, 1, far_ref)
 
 
 def whole(shape):
@@ -204,23 +220,126 @@
 
 
 def forward_rows(tiles, got, rows=8):
-    first, twr, twi, second = row_tables()
+    tables = row_tables()
+    chunks = ROWS // rows
     return pl.pallas_call(
         rows_kernel,
-        out_shape=jax.ShapeDtypeStruct((2 * PEERS, ROWS, COLS), F32),
-        grid=(ROWS // rows,),
+        out_shape=(
+            jax.ShapeDtypeStruct((80, ROWS, COLS), F32),
+            jax.ShapeDtypeStruct((48, ROWS, COLS), F32),
+        ),
+        grid=(2 * chunks,),
         in_specs=[
             pl.BlockSpec(memory_space=pltpu.SMEM),
             whole(got.shape),
-            whole(first.shape),
-            whole(twr.shape),
-            whole(twi.shape),
-            whole(second.shape),
+        ]
+        + [whole(t.shape) for t in tables],
+        out_specs=(
+            pl.BlockSpec((80, rows, COLS), lambda i: (0, jnp.minimum(i, chunks - 1), 0)),
+            pl.BlockSpec((48, rows, COLS), lambda i: (0, jnp.maximum(i - chunks, 0), 0)),
+        ),
+        scratch_shapes=[pltpu.VMEM((2 * TILES * TILE_R, TILE_C), F32)],
+        name="rows",
+    )(tiles, got, *[jnp.asarray(t) for t in tables])
+
+
+def spread_kernel(own_ref, far_ref, out_ref, send_sem, recv_sem, local_sem):
+    x, z, core = (lax.axis_index(a) for a in SLAB)
+
+    def peer(i):
+        order = i // 8
+        dz = (order + 1) // 2 * (1 - 2 * (1 - order % 2) * jnp.minimum(order, 1))
+        return (x + i // 2 % 4) % 4, (z + 8 + dz) % 8, (core + i) % 2, dz
+
+    def copy(i, far):
+        px, pz, pc, dz = peer(i)
+        reach = 1 if far else 2
+        src = far_ref if far else own_ref
+        block = ((dz + reach) * 4 + px) * 2 + pc
+        slot = x * 16 + (z + (4 if far else 0)) % 8 * 2 + core
+        return pltpu.make_async_remote_copy(
+            src_ref=src.at[block],
+            dst_ref=out_ref.at[slot],
+            send_sem=send_sem.at[i + (40 if far else 0)],
+            recv_sem=recv_sem.at[slot],
+            device_id={SLAB[0]: px, SLAB[1]: pz, SLAB[2]: pc},
+            device_id_type=pl.DeviceIdType.MESH,
+        )
+
+    def greet(i, carry):
+        px, pz, pc, _ = peer(i)
+        pl.semaphore_signal(
+            barrier,
+            inc=1,
+            device_id={SLAB[0]: px, SLAB[1]: pz, SLAB[2]: pc},
+            device_id_type=pl.DeviceIdType.MESH,
+        )
+        return carry
+
+    locals_ = []
+    for far in (False, True):
+        src, reach = (far_ref, 1) if far else (own_ref, 2)
+        slot = x * 16 + (z + (4 if far else 0)) % 8 * 2 + core
+        locals_.append(
+            pltpu.make_async_copy(
+                src.at[(reach * 4 + x) * 2 + core], out_ref.at[slot], local_sem.at[int(far)]
+            )
+        )
+        locals_[-1].start()
+    barrier = pltpu.get_barrier_semaphore()
+    lax.fori_loop(1, 40, greet, 0)
+    pl.semaphore_wait(barrier, 39)
+
+    def send(far):
+        def body(i, carry):
+            copy(i, far).start()
+            return carry
+
+        return body
+
+    lax.fori_loop(24, 40, send(False), 0)
+    lax.fori_loop(1, 24, send(False), 0)
+    lax.fori_loop(1, 24, send(True), 0)
+
+    def wait(far):
+        def body(i, carry):
+            px, pz, pc, dz = peer(i)
+            one = copy(i, far)
+            one.wait_send()
+            slot = px * 16 + (pz + (4 if far else 0)) % 8 * 2 + pc
+            pltpu.make_async_remote_copy(
+                src_ref=own_ref.at[0],
+                dst_ref=out_ref.at[slot],
+                send_sem=send_sem.at[i],
+                recv_sem=recv_sem.at[slot],
+                device_id={SLAB[0]: px, SLAB[1]: pz, SLAB[2]: pc},
+                device_id_type=pl.DeviceIdType.MESH,
+            ).wait_recv()
+            return carry
+
+        return body
+
+    lax.fori_loop(1, 40, wait(False), 0)
+    lax.fori_loop(1, 24, wait(True), 0)
+    for one in locals_:
+        one.wait()
+
+
+def spread(own, far):
+    anywhere = pl.BlockSpec(memory_space=pl.ANY)
+    return pl.pallas_call(
+        spread_kernel,
+        out_shape=jax.ShapeDtypeStruct((PEERS, 2, ROWS, COLS), F32),
+        in_specs=[anywhere, anywhere],
+        out_specs=anywhere,
+        scratch_shapes=[
+            pltpu.SemaphoreType.DMA((64,)),
+            pltpu.SemaphoreType.DMA((PEERS,)),
+            pltpu.SemaphoreType.DMA((2,)),
         ],
-        out_specs=pl.BlockSpec((2 * PEERS, rows, COLS), lambda i: (0, i, 0)),
-        scratch_shapes=[pltpu.VMEM((TILES * TILE_R, TILE_C), F32)],
-        name="rows",
-    )(tiles, got, jnp.asarray(first), jnp.asarray(twr), jnp.asarray(twi), jnp.asarray(second))
+        compiler_params=pltpu.CompilerParams(collective_id=0, has_side_effects=True),
+        name="spread",
+    )(own.reshape(40, 2, ROWS, COLS), far.reshape(24, 2, ROWS, COLS))
 
 
 STEPS = 8
@@ -418,6 +537,137 @@
     )(values, dirty, *[jnp.asarray(t) for t in tables])
 
 
+def stats_kernel(pixels, own_ref, out_ref, mine, near, far, send_sem, recv_sem):
+    chan = lax.axis_index("chan")
+    x, z, core = (lax.axis_index(a) for a in SLAB)
+
+    def near_peer(i):
+        return (z + i // 2) % 8, (core + i) % 2
+
+    def far_peer(i):
+        return (chan + i // 4) % 4, (x + i) % 4
+
+    mine[0] = jnp.concatenate(
+        [
+            jnp.sum(own_ref[:8], axis=0, keepdims=True),
+            jnp.max(own_ref[8:], axis=0, keepdims=True),
+            jnp.zeros((6, 128), F32),
+        ],
+        axis=0,
+    )
+    barrier = pltpu.get_barrier_semaphore()
+
+    def greet(i, carry):
+        pz, pc = near_peer(i)
+        pl.semaphore_signal(
+            barrier,
+            inc=1,
+            device_id={SLAB[1]: pz, SLAB[2]: pc},
+            device_id_type=pl.DeviceIdType.MESH,
+        )
+        ph, px = far_peer(i)
+        pl.semaphore_signal(
+            barrier,
+            inc=1,
+            device_id={"chan": ph, SLAB[0]: px},
+            device_id_type=pl.DeviceIdType.MESH,
+        )
+        return carry
+
+    lax.fori_loop(1, 16, greet, 0)
+    pl.semaphore_wait(barrier, 30)
+
+    def near_copy(i, slot):
+        pz, pc = near_peer(i)
+        return pltpu.make_async_remote_copy(
+            src_ref=mine.at[0],
+            dst_ref=near.at[slot],
+            send_sem=send_sem.at[i],
+            recv_sem=recv_sem.at[slot],
+            device_id={SLAB[1]: pz, SLAB[2]: pc},
+            device_id_type=pl.DeviceIdType.MESH,
+        )
+
+    def far_copy(i, slot):
+        ph, px = far_peer(i)
+        return pltpu.make_async_remote_copy(
+            src_ref=mine.at[1],
+            dst_ref=far.at[slot],
+            send_sem=send_sem.at[16 + i],
+            recv_sem=recv_sem.at[16 + slot],
+            device_id={"chan": ph, SLAB[0]: px},
+            device_id_type=pl.DeviceIdType.MESH,
+        )
+
+    def swap(copy, slot, peer_slot, store):
+        def start(i, carry):
+            copy(i, slot).start()
+            return carry
+
+        def wait(i, carry):
+            copy(i, slot).wait_send()
+            copy(i, peer_slot(i)).wait_recv()
+            return carry
+
+        lax.fori_loop(1, 16, start, 0)
+        store()
+        lax.fori_loop(1, 16, wait, 0)
+
+    def near_slot(i):
+        pz, pc = near_peer(i)
+        return pz * 2 + pc
+
+    def far_slot(i):
+        ph, px = far_peer(i)
+        return ph * 4 + px
+
+    def near_store():
+        near[z * 2 + core] = mine[0]
+
+    def far_store():
+        far[chan * 4 + x] = mine[1]
+
+    swap(near_copy, z * 2 + core, near_slot, near_store)
+    total = near[0, 0:1]
+    peak = near[0, 1:2]
+    for i in range(1, 16):
+        total = total + near[i, 0:1]
+        peak = jnp.maximum(peak, near[i, 1:2])
+    mine[1] = jnp.concatenate([total, peak, jnp.zeros((6, 128), F32)], axis=0)
+    swap(far_copy, chan * 4 + x, far_slot, far_store)
+    rows = []
+    for c in range(4):
+        total = far[4 * c, 0:1]
+        peak = far[4 * c, 1:2]
+        for i in range(1, 4):
+            total = total + far[4 * c + i, 0:1]
+            peak = jnp.maximum(peak, far[4 * c + i, 1:2])
+        root = jnp.sqrt(jnp.sum(total, axis=1, keepdims=True) * (1.0 / pixels))
+        rows.append(jnp.broadcast_to(root, (1, 128)))
+        rows.append(jnp.broadcast_to(jnp.max(peak, axis=1, keepdims=True), (1, 128)))
+    out_ref[...] = jnp.concatenate(rows, axis=0)
+
+
+def statistics(own, pixels):
+    inside = pl.BlockSpec(memory_space=pltpu.VMEM)
+    out = pl.pallas_call(
+        functools.partial(stats_kernel, pixels),
+        out_shape=jax.ShapeDtypeStruct((8, 128), F32),
+        in_specs=[inside],
+        out_specs=inside,
+        scratch_shapes=[
+            pltpu.VMEM((2, 8, 128), F32),
+            pltpu.VMEM((16, 8, 128), F32),
+            pltpu.VMEM((16, 8, 128), F32),
+            pltpu.SemaphoreType.DMA((32,)),
+            pltpu.SemaphoreType.DMA((32,)),
+        ],
+        compiler_params=pltpu.CompilerParams(collective_id=1, has_side_effects=True),
+        name="statistics",
+    )(own)
+    return out[0::2, 0], out[1::2, 0]
+
+
 def boxes(flux, offsets, counts, dest_owner, dest_tile):
     blocks, slots = offsets.shape
     live = jnp.arange(slots, dtype=jnp.int32)[None, :] < counts[:, None]
@@ -431,26 +681,24 @@
     slot = owner * 2 + rank
     marks = (slot[None, :] == jnp.arange(2 * PEERS, dtype=jnp.int32)[:, None]).astype(F32)
     box = jnp.dot(marks, payload, precision=lax.Precision.HIGHEST)
-    return box.reshape(PEERS, 4, slots)
+    box = box.reshape(4, 8, 2, 4, slots)
+    return jnp.concatenate([box, jnp.roll(box, 4, axis=1)], axis=3).reshape(PEERS, 8, slots)
 
 
 def on_device(flux, offsets, counts, dest_owner, dest_tile, dirty, psf_real, psf_imag):
     box = boxes(flux[0], offsets, counts, dest_owner, dest_tile)
     got = lax.all_to_all(box, SLAB, split_axis=0, concat_axis=0, tiled=True)
-    tiles = got.reshape(2 * PEERS, 2, -1)[:, 0, 0].astype(jnp.int32) // (TILE_R * TILE_C)
-    rows = forward_rows(tiles, got.reshape(4 * PEERS, -1))
-    rows = rows.reshape(PEERS, 2, ROWS, COLS)
-    turned = lax.all_to_all(rows, SLAB, split_axis=0, concat_axis=0, tiled=True)
+    tiles = got.reshape(PEERS, 2, 2, 2, -1)[:, :, :, 0, 0].astype(jnp.int32) // (TILE_R * TILE_C)
+    tiles = (tiles + jnp.array([0, TILES], jnp.int32)[None, :, None]).reshape(-1)
+    tiles = jnp.concatenate([tiles, lax.axis_index(SLAB[1])[None].astype(jnp.int32)])
+    own, far = forward_rows(tiles, got.reshape(8 * PEERS, -1))
+    turned = spread(own, far)
     back = columns(turned.reshape(2 * PEERS, ROWS, COLS), psf_real[0], psf_imag[0])
     back = back.reshape(PEERS, 2, ROWS, COLS)
     home = lax.all_to_all(back, SLAB, split_axis=0, concat_axis=0, tiled=True)
     residual, stats = inverse_rows(home.reshape(2 * PEERS, ROWS, COLS), dirty[0])
-    own = jnp.stack([jnp.sum(stats[:8]), jnp.max(stats[8:])])
-    every = lax.all_gather(own[None], ("chan",) + SLAB, axis=0, tiled=True)
-    every = every.reshape(-1, PEERS, 2)
-    pixel_total = PEERS * dirty.shape[1] * dirty.shape[2]
-    rms_values = jnp.sqrt(jnp.sum(every[:, :, 0], axis=1) / pixel_total)
-    peak_values = jnp.max(every[:, :, 1], axis=1)
+    pixels = PEERS * dirty.shape[1] * dirty.shape[2]
+    rms_values, peak_values = statistics(stats, pixels)
     return residual[None], rms_values, peak_values
 
 

time: 381 us -> 299 us (0.78)
  blocking collectives: 201 us -> 104 us
  Pallas kernels: 66.2 us -> 160 us
  waiting for transfers between devices: 95.8 us -> 11.7 us
  starting transfers between devices: 6.03 us -> 13 us
  other arithmetic: 10.8 us -> 6.57 us
    pallas_call x1 -> x3, Pallas kernels: 16.9 us -> 111 us  [the longest x1 62.2 us: spread(): pl.pallas_call(spread_kernel, out_shape=jax.ShapeDtypeStruct((PEERS, 2, R...]
    all_to_all x1, waiting for transfers between devices: 95.8 us -> 11.7 us  [on_device(): got = lax.all_to_all(box, SLAB, split_axis=0, concat_axis=0, tiled=True)]
    unnamed x1 -> x0, blocking collectives: 76 us -> none
    all_to_all x2 -> x1, blocking collectives: 125 us -> 104 us  [on_device(): home = lax.all_to_all(back, SLAB, split_axis=0, concat_axis=0, tiled=True)]
    all_to_all x1, starting transfers between devices: 6.03 us -> 13 us  [on_device(): got = lax.all_to_all(box, SLAB, split_axis=0, concat_axis=0, tiled=True)]
where the time goes in v2:
time: 299 us
  Pallas kernels  160 us (54%)
  blocking collectives  104 us (35%)
  starting transfers between devices  13 us (4%)
  waiting for transfers between devices  11.7 us (4%)
  other arithmetic  6.57 us (2%)
    all_to_all x1, blocking collectives, on_device(): home = lax.all_to_all(back, SLAB, split_axis=0, concat_axis=0, tiled=True)  104 us
    pallas_call x1, Pallas kernels, spread(): pl.pallas_call(spread_kernel, out_shape=jax.ShapeDtypeStruct((PEERS, 2, R...  62.2 us
    pallas_call x1, Pallas kernels, columns(): pl.pallas_call(columns_kernel, out_shape=jax.ShapeDtypeStruct((128, ROWS,...  39.5 us
    pallas_call x1, Pallas kernels, forward_rows(): pl.pallas_call(rows_kernel, out_shape=(jax.ShapeDtypeStruct((80, ROWS, CO...  31.8 us
    pallas_call x1, Pallas kernels, statistics(): pl.pallas_call(functools.partial(stats_kernel, pixels), out_shape=jax.Sha...  16.6 us
    all_to_all x1, starting transfers between devices, on_device(): got = lax.all_to_all(box, SLAB, split_axis=0, concat_axis=0, tiled=True)  13 us
    all_to_all x1, waiting for transfers between devices, on_device(): got = lax.all_to_all(box, SLAB, split_axis=0, concat_axis=0, tiled=True)  11.7 us
    pallas_call x1, Pallas kernels, inverse_rows(): pl.pallas_call(inverse_kernel, out_shape=(jax.ShapeDtypeStruct((ROWS, wid...  9.87 us
  transfers between devices with their start and end apart: 1, of which 1 were waited for; matrix products, arithmetic and copies ran while one was open for 0% of the time, Pallas kernels for 0%

profile of v2, /device:TPU:1, one launch (start us, length us, event | category | flops | bytes accessed | tf_op | source)
XLA Modules:
  0.0 298.5 jit_solution(17914504995750255726)
XLA Ops:
  0.6 0.7 broadcast_multiply_fusion
  1.3 0.9 convert_reduce_fusion
  2.2 0.7 multiply_add_fusion
  2.9 0.8 add_convert_fusion
  3.7 0.8 bitcast_select_fusion
  4.5 0.2 fusion
  4.9 0.8 pad_maximum_fusion
  5.7 13.0 %all-to-all-start = ((f32[64,8,128]{2,1,0:T(8,128)}), f32[64,8,128]{2,1,0:T(8,128)S(1)}, u32[]{:S(2)}, u32[]{:S(2)}) async-start(f32[64,8,128]{2,1,0:T(8,128)} %pad_maximum_fusion), calls=%async_computation | async-start | bytes 524288 | tf_op jit(solution)/shard_map/all_to_all | solution.py:690
  18.8 0.1 add.32
  18.9 11.7 %all-to-all-done = f32[64,8,128]{2,1,0:T(8,128)S(1)} async-done(((f32[64,8,128]{2,1,0:T(8,128)}), f32[64,8,128]{2,1,0:T(8,128)S(1)}, u32[]{:S(2)}, u32[]{:S(2)}) %all-to-all-start) | async-done | bytes 262176 | tf_op jit(solution)/shard_map/all_to_all | solution.py:690
  30.8 0.1 copy.44
  30.9 0.1 copy.41
  31.0 0.2 convert_element_type.17
  31.2 0.6 pad_add_fusion.tile_ref
  31.8 31.8 %rows.1 = (f32[80,64,128]{2,1,0:T(8,128)}, f32[48,64,128]{2,1,0:T(8,128)}) custom-call(s32[257]{0:T(512)} %pad_add_fusion.tile_ref, f32[512,128]{1,0:T(8,128)} %bitcast.26, bf16[256,96]{1,0:T(8,128)(2,1)} %constant.69.clone.first_ref, f32[128,128]{1,0:T(8,128)} %constant.70.clone.twr_ref, f32[128,128]{1,0:T(8,128)} %constant.71.clone.twi_ref, ...), custom_call_target="tpu_custom_call" | custom-call | tf_op jit(solution)/shard_map/rows/pallas_call | solution.py:225
  63.6 62.2 %spread.1 = f32[64,2,64,128]{3,2,1,0:T(8,128)} custom-call(f32[40,2,64,128]{3,2,1,0:T(8,128)} %bitcast.24, f32[24,2,64,128]{3,2,1,0:T(8,128)} %bitcast.27), custom_call_target="tpu_custom_call" | custom-call | tf_op jit(solution)/shard_map/spread/pallas_call | solution.py:330
  125.8 39.5 %columns.1 = f32[128,64,128]{2,1,0:T(8,128)} custom-call(f32[128,64,128]{2,1,0:T(8,128)} %bitcast.20, f32[64,128,128]{2,1,0:T(8,128)} %bitcast.22, f32[64,128,128]{2,1,0:T(8,128)} %bitcast.23, bf16[256,256]{1,0:T(8,128)(2,1)} %constant.74.clone.first_ref, bf16[256,128]{1,0:T(8,128)(2,1)} %constant.75.clone.first_lo_ref, ...), custom_call_target="tpu_custom_call" | custom-call | tf_op jit(solution)/shard_map/columns/pallas_call | solution.py:444
  165.2 104.2 %all_to_all.10 = f32[64,2,64,128]{3,2,1,0:T(8,128)} all-to-all(f32[64,2,64,128]{3,2,1,0:T(8,128)} %bitcast.21), channel_id=1, replica_groups=mesh['chan'=4,'slab_0'=4,'slab_1'=8,'slab_2'=2] {'slab_0','slab_1','slab..., dimensions={0} | all-to-all | bytes 8388608 | tf_op jit(solution)/shard_map/all_to_all | solution.py:698
  269.4 9.9 %inverse.1 = (f32[64,4096]{1,0:T(8,128)}, f32[16,128]{1,0:T(8,128)}) custom-call(f32[128,64,128]{2,1,0:T(8,128)} %bitcast.19, f32[64,4096]{1,0:T(8,128)} %bitcast.28, bf16[128,256]{1,0:T(8,128)(2,1)} %constant.83.clone.first_ref, bf16[128,128]{1,0:T(8,128)(2,1)} %constant.84.clone.first_lo_ref, f32[128,128]{1,0:T(8,128)} %constant.70.clone.twr_ref, ...), custom_call_target="tpu_custom_call" | custom-call | tf_op jit(solution)/shard_map/inverse/pallas_call | solution.py:519
  279.3 16.6 %statistics.1 = f32[8,128]{1,0:T(8,128)} custom-call(f32[16,128]{1,0:T(8,128)} %get-tuple-element.10.own_ref), custom_call_target="tpu_custom_call" | custom-call | tf_op jit(solution)/shard_map/statistics/pallas_call | solution.py:653
  295.9 0.7 slice.21
  296.6 0.7 slice.20
  297.3 0.6 reduce
  297.9 0.6 reduce.1
  (11 shorter events, 0.4 us)
Async XLA Ops:
  5.7 24.9 %all-to-all-start = ((f32[64,8,128]{2,1,0:T(8,128)}), f32[64,8,128]{2,1,0:T(8,128)S(1)}, u32[]{:S(2)}, u32[]{:S(2)}) async-start(f32[64,8,128]{2,1,0:T(8,128)} %pad_maximum_fusion), calls=%async_computation | async-start | bytes 524288 | tf_op jit(solution)/shard_map/all_to_all | solution.py:690
  30.7 1.1 copy-start

commit v3 on v2

--- a/solution.py
+++ b/solution.py
@@ -69,12 +69,6 @@
     c, s = np.cos(angle), np.sin(angle)
     third_hi, third_lo = halves(np.block([[c, -s], [s, c]]))
     third = np.concatenate([third_hi, third_lo], axis=1)
-    angle = turns(a, k, 128)
-    c, s = np.cos(angle) * 2.0**-26, np.sin(angle) * 2.0**-26
-    fourth = np.stack([np.stack([c, -s], axis=2), np.stack([s, c], axis=2)], axis=1)
-    fourth_turn = np.stack([np.stack([-s, -c], axis=2), np.stack([c, -s], axis=2)], axis=1)
-    angle = np.repeat(turns(b, k, LENGTH), 2, axis=1)
-    last_phase = np.stack([np.cos(angle), np.sin(angle)], axis=1)
     return (
         np.concatenate([first_hi, first_hi], axis=1),
         first_lo,
@@ -82,6 +76,18 @@
         second_turn,
         phase.astype(np.float32),
         third,
+    )
+
+
+def back_tables():
+    r1, k, r0 = np.arange(64), np.arange(128), np.arange(64)
+    angle = turns(r1, k, 128)
+    c, s = np.cos(angle) * 2.0**-26, np.sin(angle) * 2.0**-26
+    fourth = np.stack([np.stack([c, -s], axis=2), np.stack([s, c], axis=2)], axis=1)
+    fourth_turn = np.stack([np.stack([-s, -c], axis=2), np.stack([c, -s], axis=2)], axis=1)
+    angle = np.repeat(turns(r0, k, LENGTH), 2, axis=1)
+    last_phase = np.stack([np.cos(angle), np.sin(angle)], axis=1)
+    return (
         fourth.reshape(128, 256).astype(np.float32),
         fourth_turn.reshape(128, 256).astype(np.float32),
         last_phase.astype(np.float32),
@@ -343,6 +349,7 @@
 
 
 STEPS = 8
+UNROLL = 4
 
 
 def columns_kernel(
@@ -355,9 +362,6 @@
     second_turn_ref,
     phase_ref,
     third_ref,
-    fourth_ref,
-    fourth_turn_ref,
-    last_phase_ref,
     out_ref,
     held,
 ):
@@ -379,10 +383,12 @@
                 at = pl.multiple_of((step * rows + 2 * pair + e) * 256, 256)
                 held[pl.ds(at, 256), :] = result[:, e * COLS : (e + 1) * COLS]
 
-    @pl.when(jnp.logical_and(step >= STEPS, step < 2 * STEPS))
+    @pl.when(step >= STEPS)
     def _():
         pr = pr_ref.reshape(64 * per, COLS)
         pi = pi_ref.reshape(64 * per, COLS)
+
+        out = out_ref.reshape(64 * 2 * per, COLS)
 
         def body(i, carry):
             k = (step - STEPS) * per + i
@@ -408,27 +414,10 @@
             third = third_ref[...]
             result = mm(third, jnp.concatenate([high, high], axis=0)) + mm(third[:, :128], low)
             for s in range(2):
-                held[pl.ds(2 * k + s, 64, stride=256), :] = result[64 * s : 64 * s + 64]
-            return carry
-
-        lax.fori_loop(0, per, body, 0, unroll=4)
-
-    @pl.when(step >= 2 * STEPS)
-    def _():
-        out = out_ref.reshape(128 * rows, COLS)
-        for pair in range(rows // 2):
-            for e in range(2):
-                row = (step - 2 * STEPS) * rows + 2 * pair + e
-                table = (
-                    fourth_ref[...] * last_phase_ref[row, 0:1, :]
-                    + fourth_turn_ref[...] * last_phase_ref[row, 1:2, :]
-                )
-                table_hi, table_lo = split(table)
-                at = pl.multiple_of(row * 256, 256)
-                high, low = split(held[pl.ds(at, 256), :])
-                full = mm(jnp.concatenate([table_hi, table_lo], axis=0), high)
-                result = full[:128] + full[128:] + mm(table_hi, low)
-                out[pl.ds(2 * pair + e, 128, stride=rows), :] = result
+                out[pl.ds(2 * i + s, 64, stride=2 * per), :] = result[64 * s : 64 * s + 64]
+            return carry
+
+        lax.fori_loop(0, per, body, 0, unroll=UNROLL)
 
 
 def columns(values, psf_re, psf_im):
@@ -438,234 +427,319 @@
     psf_re = psf_re.reshape(64, 128, COLS)
     psf_im = psf_im.reshape(64, 128, COLS)
 
-    def psf_at(i):
-        return (0, jnp.clip(i - STEPS, 0, STEPS - 1), 0)
+    def later(i):
+        return (0, jnp.maximum(i - STEPS, 0), 0)
 
     return pl.pallas_call(
         columns_kernel,
-        out_shape=jax.ShapeDtypeStruct((128, ROWS, COLS), F32),
-        grid=(3 * STEPS,),
+        out_shape=jax.ShapeDtypeStruct((64, 256, COLS), F32),
+        grid=(2 * STEPS,),
         in_specs=[
             pl.BlockSpec((128, rows, COLS), lambda i: (0, jnp.minimum(i, STEPS - 1), 0)),
-            pl.BlockSpec((64, per, COLS), psf_at),
-            pl.BlockSpec((64, per, COLS), psf_at),
+            pl.BlockSpec((64, per, COLS), later),
+            pl.BlockSpec((64, per, COLS), later),
         ]
         + [whole(t.shape) for t in tables],
-        out_specs=pl.BlockSpec(
-            (128, rows, COLS), lambda i: (0, jnp.maximum(i - 2 * STEPS, 0), 0)
-        ),
+        out_specs=pl.BlockSpec((64, 2 * per, COLS), later),
         scratch_shapes=[pltpu.VMEM((64 * 256, COLS), F32)],
         name="columns",
     )(values, psf_re, psf_im, *[jnp.asarray(t) for t in tables])
 
 
-def inverse_kernel(
-    y_ref, dirty_ref, first_ref, first_lo_ref, twr_ref, twi_ref, last_ref, out_ref, stat_ref, smear
+CHUNKS = 4
+PART = ROWS // CHUNKS
+MESH = pl.DeviceIdType.MESH
+
+
+def back_kernel(
+    pixels,
+    v_ref,
+    dirty_ref,
+    fourth_ref,
+    fourth_turn_ref,
+    last_phase_ref,
+    first_ref,
+    first_lo_ref,
+    twr_ref,
+    twi_ref,
+    last_ref,
+    out_ref,
+    rms_ref,
+    peak_ref,
+    v_buf,
+    y_buf,
+    in_buf,
+    smear,
+    mine,
+    near,
+    far,
+    v_sem,
+    send_sem,
+    recv_sem,
+    own_sem,
+    near_send,
+    near_recv,
+    far_send,
+    far_recv,
 ):
-    step = pl.program_id(0)
-    rows = y_ref.shape[1]
-    y = y_ref.reshape(128 * rows, COLS)
-    for pair in range(rows // 2):
-        values = jnp.concatenate(
-            [y[pl.ds(2 * pair + e, 128, stride=rows), :] for e in range(2)], axis=1
-        )
-        high, low = split(values)
-        partial = mm(first_ref[...], jnp.concatenate([high, low], axis=0)) + mm(
-            first_lo_ref[...], high
-        )
-        turned = []
-        for e in range(2):
-            re = partial[:64, e * COLS : (e + 1) * COLS]
-            im = partial[64:, e * COLS : (e + 1) * COLS]
-            re = jnp.concatenate([re, re], axis=0)
-            im = jnp.concatenate([im, im], axis=0)
-            turned.append(
-                jnp.concatenate(
-                    [
-                        re * twr_ref[...] - im * twi_ref[...],
-                        re * twi_ref[...] + im * twr_ref[...],
-                    ],
-                    axis=1,
-                )
-            )
-        high, low = split(jnp.concatenate(turned, axis=0))
-        full = mm_nt(last_ref[...], high)
-        result = full[:TILES] + full[TILES:] + mm_nt(last_ref[:TILES], low)
-        for e in range(2):
-            smear[pl.ds(2 * pair + e, TILES, stride=rows), :] = result[
-                :, e * TILE_C : (e + 1) * TILE_C
-            ]
-    squares = jnp.zeros((rows, TILE_C), F32)
-    peaks = jnp.zeros((rows, TILE_C), F32)
-    for t in range(TILES):
-        lanes = slice(t * TILE_C, (t + 1) * TILE_C)
-        rest = dirty_ref[:, lanes] - smear[t * rows : (t + 1) * rows, :]
-        out_ref[:, lanes] = rest
-        squares += rest * rest
-        peaks = jnp.maximum(peaks, jnp.abs(rest))
-
-    @pl.when(step == 0)
-    def _():
-        stat_ref[...] = jnp.zeros_like(stat_ref)
-
-    stat_ref[0:8, :] += squares
-    stat_ref[8:16, :] = jnp.maximum(stat_ref[8:16, :], peaks)
-
-
-def inverse_rows(values, dirty):
-    tables = inverse_tables()
-    rows = 8
-    width = dirty.shape[1]
-    return pl.pallas_call(
-        inverse_kernel,
-        out_shape=(
-            jax.ShapeDtypeStruct((ROWS, width), F32),
-            jax.ShapeDtypeStruct((16, TILE_C), F32),
-        ),
-        grid=(ROWS // rows,),
-        in_specs=[
-            pl.BlockSpec((128, rows, COLS), lambda i: (0, i, 0)),
-            pl.BlockSpec((rows, width), lambda i: (i, 0)),
-        ]
-        + [whole(t.shape) for t in tables],
-        out_specs=(
-            pl.BlockSpec((rows, width), lambda i: (i, 0)),
-            pl.BlockSpec((16, TILE_C), lambda i: (0, 0)),
-        ),
-        scratch_shapes=[pltpu.VMEM((TILES * rows, TILE_C), F32)],
-        name="inverse",
-    )(values, dirty, *[jnp.asarray(t) for t in tables])
-
-
-def stats_kernel(pixels, own_ref, out_ref, mine, near, far, send_sem, recv_sem):
     chan = lax.axis_index("chan")
     x, z, core = (lax.axis_index(a) for a in SLAB)
-
-    def near_peer(i):
-        return (z + i // 2) % 8, (core + i) % 2
+    me = x * 16 + z * 2 + core
+    fetches = [
+        pltpu.make_async_copy(v_ref.at[pl.ds(c * PART, PART)], v_buf.at[c], v_sem.at[c])
+        for c in range(CHUNKS)
+    ]
+    for fetch in fetches:
+        fetch.start()
+    barrier = pltpu.get_barrier_semaphore()
+
+    def peer(i):
+        turn = i % 8
+        dz = (turn + 1) // 2 * (1 - 2 * (1 - turn % 2)) + 8
+        return (x + i // 16) % 4, (z + dz) % 8, (core + i // 8) % 2
+
+    def where(i):
+        px, pz, pc = peer(i)
+        return {SLAB[0]: px, SLAB[1]: pz, SLAB[2]: pc}
+
+    def greet(i, carry):
+        pl.semaphore_signal(barrier, inc=1, device_id=where(i), device_id_type=MESH)
+        return carry
 
     def far_peer(i):
-        return (chan + i // 4) % 4, (x + i) % 4
-
-    mine[0] = jnp.concatenate(
-        [
-            jnp.sum(own_ref[:8], axis=0, keepdims=True),
-            jnp.max(own_ref[8:], axis=0, keepdims=True),
-            jnp.zeros((6, 128), F32),
-        ],
-        axis=0,
-    )
-    barrier = pltpu.get_barrier_semaphore()
-
-    def greet(i, carry):
-        pz, pc = near_peer(i)
-        pl.semaphore_signal(
-            barrier,
-            inc=1,
-            device_id={SLAB[1]: pz, SLAB[2]: pc},
-            device_id_type=pl.DeviceIdType.MESH,
-        )
+        return (chan + 1 + i // 4) % 4, (x + i) % 4
+
+    def greet_far(i, carry):
         ph, px = far_peer(i)
         pl.semaphore_signal(
-            barrier,
-            inc=1,
-            device_id={"chan": ph, SLAB[0]: px},
-            device_id_type=pl.DeviceIdType.MESH,
+            barrier, inc=1, device_id={"chan": ph, SLAB[0]: px}, device_id_type=MESH
         )
         return carry
 
-    lax.fori_loop(1, 16, greet, 0)
-    pl.semaphore_wait(barrier, 30)
+    lax.fori_loop(1, PEERS, greet, 0)
+    lax.fori_loop(0, 12, greet_far, 0)
+
+    def produce(c):
+        def body(g, carry):
+            for e in range(4):
+                i = g * 4 + e
+                table = (
+                    fourth_ref[...] * last_phase_ref[c * PART + i, 0:1, :]
+                    + fourth_turn_ref[...] * last_phase_ref[c * PART + i, 1:2, :]
+                )
+                table_hi, table_lo = split(table)
+                high, low = split(v_buf[c, i])
+                full = mm(jnp.concatenate([table_hi, table_lo], axis=0), high)
+                result = full[:128] + full[128:] + mm(table_hi, low)
+                y_buf[c, pl.ds(i, 128, stride=PART), :] = result
+            return carry
+
+        fetches[c].wait()
+        lax.fori_loop(0, PART // 4, body, 0)
+
+    span = 2 * PART
+
+    def block(slot):
+        return pl.ds(pl.multiple_of(slot * span, span), span)
+
+    def send(c):
+        pltpu.make_async_copy(
+            y_buf.at[c, block(me)], in_buf.at[c, block(me)], own_sem.at[c]
+        ).start()
+
+        def body(i, carry):
+            px, pz, pc = peer(i)
+            pltpu.make_async_remote_copy(
+                src_ref=y_buf.at[c, block(px * 16 + pz * 2 + pc)],
+                dst_ref=in_buf.at[c, block(me)],
+                send_sem=send_sem.at[c],
+                recv_sem=recv_sem.at[c],
+                device_id=where(i),
+                device_id_type=MESH,
+            ).start()
+            return carry
+
+        lax.fori_loop(1, PEERS, body, 0)
+
+    def collect(c):
+        others = pl.ds(0, (PEERS - 1) * span)
+        pltpu.make_async_copy(
+            in_buf.at[c, others], in_buf.at[c, others], recv_sem.at[c]
+        ).wait()
+        pltpu.make_async_copy(
+            y_buf.at[c, block(me)], in_buf.at[c, block(me)], own_sem.at[c]
+        ).wait()
+
+    def consume(c):
+        def body(pair, carry):
+            values = jnp.concatenate(
+                [in_buf[c, pl.ds(2 * pair + e, 128, stride=PART), :] for e in range(2)], axis=1
+            )
+            high, low = split(values)
+            partial = mm(first_ref[...], jnp.concatenate([high, low], axis=0)) + mm(
+                first_lo_ref[...], high
+            )
+            turned = []
+            for e in range(2):
+                re = partial[:64, e * COLS : (e + 1) * COLS]
+                im = partial[64:, e * COLS : (e + 1) * COLS]
+                re = jnp.concatenate([re, re], axis=0)
+                im = jnp.concatenate([im, im], axis=0)
+                turned.append(
+                    jnp.concatenate(
+                        [
+                            re * twr_ref[...] - im * twi_ref[...],
+                            re * twi_ref[...] + im * twr_ref[...],
+                        ],
+                        axis=1,
+                    )
+                )
+            high, low = split(jnp.concatenate(turned, axis=0))
+            full = mm_nt(last_ref[...], high)
+            result = full[:TILES] + full[TILES:] + mm_nt(last_ref[:TILES], low)
+            for e in range(2):
+                smear[pl.ds(2 * pair + e, TILES, stride=PART), :] = result[
+                    :, e * TILE_C : (e + 1) * TILE_C
+                ]
+            return carry
+
+        lax.fori_loop(0, PART // 2, body, 0, unroll=2)
+        squares = jnp.zeros((PART, TILE_C), F32)
+        peaks = jnp.zeros((PART, TILE_C), F32)
+        for t in range(TILES):
+            at = (slice(c * PART, (c + 1) * PART), slice(t * TILE_C, (t + 1) * TILE_C))
+            rest = dirty_ref[at] - smear[t * PART : (t + 1) * PART, :]
+            out_ref[at] = rest
+            squares += rest * rest
+            peaks = jnp.maximum(peaks, jnp.abs(rest))
+        return (
+            jnp.sum(squares, axis=0, keepdims=True),
+            jnp.max(peaks, axis=0, keepdims=True),
+        )
+
+    produce(0)
+    pl.semaphore_wait(barrier, PEERS - 1 + 12)
+    send(0)
+    for c in range(1, CHUNKS):
+        produce(c)
+        if c > 1:
+            send(c - 1)
+    collect(0)
+    send(CHUNKS - 1)
+    total, peak = consume(0)
+    for c in range(1, CHUNKS):
+        collect(c)
+        one, top = consume(c)
+        total, peak = total + one, jnp.maximum(peak, top)
+    for c in range(CHUNKS):
+        others = pl.ds(0, (PEERS - 1) * span)
+        pltpu.make_async_copy(y_buf.at[c, others], y_buf.at[c, others], send_sem.at[c]).wait()
+
+    filler = jnp.zeros((6, 128), F32)
+    mine[0] = jnp.concatenate([total, peak, filler], axis=0)
 
     def near_copy(i, slot):
-        pz, pc = near_peer(i)
         return pltpu.make_async_remote_copy(
             src_ref=mine.at[0],
             dst_ref=near.at[slot],
-            send_sem=send_sem.at[i],
-            recv_sem=recv_sem.at[slot],
-            device_id={SLAB[1]: pz, SLAB[2]: pc},
-            device_id_type=pl.DeviceIdType.MESH,
+            send_sem=near_send.at[i],
+            recv_sem=near_recv.at[slot],
+            device_id={SLAB[1]: (z + i // 2) % 8, SLAB[2]: (core + i) % 2},
+            device_id_type=MESH,
         )
 
     def far_copy(i, slot):
-        ph, px = far_peer(i)
         return pltpu.make_async_remote_copy(
             src_ref=mine.at[1],
             dst_ref=far.at[slot],
-            send_sem=send_sem.at[16 + i],
-            recv_sem=recv_sem.at[16 + slot],
-            device_id={"chan": ph, SLAB[0]: px},
-            device_id_type=pl.DeviceIdType.MESH,
+            send_sem=far_send.at[i],
+            recv_sem=far_recv.at[slot],
+            device_id={"chan": (chan + i // 4) % 4, SLAB[0]: (x + i) % 4},
+            device_id_type=MESH,
         )
 
-    def swap(copy, slot, peer_slot, store):
+    def near_slot(i):
+        return (z + i // 2) % 8 * 2 + (core + i) % 2
+
+    def far_slot(i):
+        return (chan + i // 4) % 4 * 4 + (x + i) % 4
+
+    def swap(copy, slot_of):
         def start(i, carry):
-            copy(i, slot).start()
-            return carry
-
+            copy(i, slot_of(0)).start()
+            return carry
+
+        lax.fori_loop(1, 16, start, 0)
+
+    def settle(copy, slot_of):
         def wait(i, carry):
-            copy(i, slot).wait_send()
-            copy(i, peer_slot(i)).wait_recv()
-            return carry
-
-        lax.fori_loop(1, 16, start, 0)
-        store()
+            copy(i, slot_of(0)).wait_send()
+            copy(i, slot_of(i)).wait_recv()
+            return carry
+
         lax.fori_loop(1, 16, wait, 0)
 
-    def near_slot(i):
-        pz, pc = near_peer(i)
-        return pz * 2 + pc
-
-    def far_slot(i):
-        ph, px = far_peer(i)
-        return ph * 4 + px
-
-    def near_store():
-        near[z * 2 + core] = mine[0]
-
-    def far_store():
-        far[chan * 4 + x] = mine[1]
-
-    swap(near_copy, z * 2 + core, near_slot, near_store)
+    swap(near_copy, near_slot)
+    near[near_slot(0)] = mine[0]
+    settle(near_copy, near_slot)
     total = near[0, 0:1]
     peak = near[0, 1:2]
     for i in range(1, 16):
         total = total + near[i, 0:1]
         peak = jnp.maximum(peak, near[i, 1:2])
-    mine[1] = jnp.concatenate([total, peak, jnp.zeros((6, 128), F32)], axis=0)
-    swap(far_copy, chan * 4 + x, far_slot, far_store)
-    rows = []
-    for c in range(4):
-        total = far[4 * c, 0:1]
-        peak = far[4 * c, 1:2]
+    mine[1] = jnp.concatenate([total, peak, filler], axis=0)
+    swap(far_copy, far_slot)
+    far[far_slot(0)] = mine[1]
+    settle(far_copy, far_slot)
+    lane = lax.broadcasted_iota(jnp.int32, (1, 128), 1)
+    roots = jnp.zeros((1, 128), F32)
+    tops = jnp.zeros((1, 128), F32)
+    for h in range(4):
+        total = far[4 * h, 0:1]
+        peak = far[4 * h, 1:2]
         for i in range(1, 4):
-            total = total + far[4 * c + i, 0:1]
-            peak = jnp.maximum(peak, far[4 * c + i, 1:2])
-        root = jnp.sqrt(jnp.sum(total, axis=1, keepdims=True) * (1.0 / pixels))
-        rows.append(jnp.broadcast_to(root, (1, 128)))
-        rows.append(jnp.broadcast_to(jnp.max(peak, axis=1, keepdims=True), (1, 128)))
-    out_ref[...] = jnp.concatenate(rows, axis=0)
-
-
-def statistics(own, pixels):
+            total = total + far[4 * h + i, 0:1]
+            peak = jnp.maximum(peak, far[4 * h + i, 1:2])
+        mean = jnp.sum(total, axis=1, keepdims=True) * (1.0 / pixels)
+        roots = jnp.where(lane == h, jnp.sqrt(mean), roots)
+        tops = jnp.where(lane == h, jnp.max(peak, axis=1, keepdims=True), tops)
+    rms_ref[...] = roots
+    peak_ref[...] = tops
+
+
+def back(values, dirty, pixels):
+    tables = back_tables() + inverse_tables()
     inside = pl.BlockSpec(memory_space=pltpu.VMEM)
-    out = pl.pallas_call(
-        functools.partial(stats_kernel, pixels),
-        out_shape=jax.ShapeDtypeStruct((8, 128), F32),
-        in_specs=[inside],
-        out_specs=inside,
+    residual, rms, peaks = pl.pallas_call(
+        functools.partial(back_kernel, pixels),
+        out_shape=(
+            jax.ShapeDtypeStruct(dirty.shape, F32),
+            jax.ShapeDtypeStruct((1, 128), F32),
+            jax.ShapeDtypeStruct((1, 128), F32),
+        ),
+        in_specs=[pl.BlockSpec(memory_space=pl.ANY)] + [inside] * (1 + len(tables)),
+        out_specs=(inside, inside, inside),
         scratch_shapes=[
+            pltpu.VMEM((CHUNKS, PART, 256, COLS), F32),
+            pltpu.VMEM((CHUNKS, 2 * PEERS * PART, COLS), F32),
+            pltpu.VMEM((CHUNKS, 2 * PEERS * PART, COLS), F32),
+            pltpu.VMEM((TILES * PART, TILE_C), F32),
             pltpu.VMEM((2, 8, 128), F32),
             pltpu.VMEM((16, 8, 128), F32),
             pltpu.VMEM((16, 8, 128), F32),
-            pltpu.SemaphoreType.DMA((32,)),
-            pltpu.SemaphoreType.DMA((32,)),
+            pltpu.SemaphoreType.DMA((CHUNKS,)),
+            pltpu.SemaphoreType.DMA((CHUNKS,)),
+            pltpu.SemaphoreType.DMA((CHUNKS,)),
+            pltpu.SemaphoreType.DMA((CHUNKS,)),
+            pltpu.SemaphoreType.DMA((16,)),
+            pltpu.SemaphoreType.DMA((16,)),
+            pltpu.SemaphoreType.DMA((16,)),
+            pltpu.SemaphoreType.DMA((16,)),
         ],
         compiler_params=pltpu.CompilerParams(collective_id=1, has_side_effects=True),
-        name="statistics",
-    )(own)
-    return out[0::2, 0], out[1::2, 0]
+        name="back",
+    )(values, dirty, *[jnp.asarray(t) for t in tables])
+    return residual, rms[0, :4], peaks[0, :4]
 
 
 def boxes(flux, offsets, counts, dest_owner, dest_tile):
@@ -693,12 +767,9 @@
     tiles = jnp.concatenate([tiles, lax.axis_index(SLAB[1])[None].astype(jnp.int32)])
     own, far = forward_rows(tiles, got.reshape(8 * PEERS, -1))
     turned = spread(own, far)
-    back = columns(turned.reshape(2 * PEERS, ROWS, COLS), psf_real[0], psf_imag[0])
-    back = back.reshape(PEERS, 2, ROWS, COLS)
-    home = lax.all_to_all(back, SLAB, split_axis=0, concat_axis=0, tiled=True)
-    residual, stats = inverse_rows(home.reshape(2 * PEERS, ROWS, COLS), dirty[0])
+    values = columns(turned.reshape(2 * PEERS, ROWS, COLS), psf_real[0], psf_imag[0])
     pixels = PEERS * dirty.shape[1] * dirty.shape[2]
-    rms_values, peak_values = statistics(stats, pixels)
+    residual, rms_values, peak_values = back(values, dirty[0], pixels)
     return residual[None], rms_values, peak_values
 
 

time: 299 us -> 281 us (0.940)
  blocking collectives: 104 us -> 0 us
  Pallas kernels: 160 us -> 245 us
    all_to_all x1 -> x0, blocking collectives: 104 us -> none  [on_device(): home = lax.all_to_all(back, SLAB, split_axis=0, concat_axis=0, tiled=True)]
    pallas_call x3 -> x2, Pallas kernels: 65.9 us -> 152 us  [the longest x1 118 us: back(): pl.pallas_call(functools.partial(back_kernel, pixels), out_shape=(jax.Sha...]
where the time goes in v3:
time: 281 us
  Pallas kernels  245 us (87%)
  starting transfers between devices  13 us (5%)
  waiting for transfers between devices  11.7 us (4%)
  other arithmetic  5.32 us (2%)
  local copies, waits for them, and re-layouts  4.24 us (2%)
    pallas_call x1, Pallas kernels, back(): pl.pallas_call(functools.partial(back_kernel, pixels), out_shape=(jax.Sha...  118 us
    pallas_call x1, Pallas kernels, spread(): pl.pallas_call(spread_kernel, out_shape=jax.ShapeDtypeStruct((PEERS, 2, R...  62 us
    pallas_call x1, Pallas kernels, columns(): pl.pallas_call(columns_kernel, out_shape=jax.ShapeDtypeStruct((64, 256, C...  33.6 us
    pallas_call x1, Pallas kernels, forward_rows(): pl.pallas_call(rows_kernel, out_shape=(jax.ShapeDtypeStruct((80, ROWS, CO...  31.9 us
    all_to_all x1, starting transfers between devices, on_device(): got = lax.all_to_all(box, SLAB, split_axis=0, concat_axis=0, tiled=True)  13 us
    all_to_all x1, waiting for transfers between devices, on_device(): got = lax.all_to_all(box, SLAB, split_axis=0, concat_axis=0, tiled=True)  11.7 us
  transfers between devices with their start and end apart: 1, of which 1 were waited for; matrix products, arithmetic and copies ran while one was open for 0% of the time, Pallas kernels for 0%

profile of v3, /device:TPU:1, one launch (start us, length us, event | category | flops | bytes accessed | tf_op | source)
XLA Modules:
  0.0 280.6 jit_solution(8129441936446338987)
XLA Ops:
  0.6 0.7 broadcast_multiply_fusion
  1.3 0.9 convert_reduce_fusion
  2.2 0.7 multiply_add_fusion
  2.9 0.8 add_convert_fusion
  3.7 0.8 bitcast_select_fusion
  4.5 0.2 fusion
  4.7 0.1 reshape.45
  4.8 0.1 concatenate.19
  4.9 0.8 pad_maximum_fusion
  5.7 13.0 %all-to-all-start = ((f32[64,8,128]{2,1,0:T(8,128)}), f32[64,8,128]{2,1,0:T(8,128)S(1)}, u32[]{:S(2)}, u32[]{:S(2)}) async-start(f32[64,8,128]{2,1,0:T(8,128)} %pad_maximum_fusion), calls=%async_computation | async-start | bytes 524288 | tf_op jit(solution)/shard_map/all_to_all | solution.py:764
  18.7 0.1 add.31
  18.8 0.1 add.32
  18.9 11.7 %all-to-all-done = f32[64,8,128]{2,1,0:T(8,128)S(1)} async-done(((f32[64,8,128]{2,1,0:T(8,128)}), f32[64,8,128]{2,1,0:T(8,128)S(1)}, u32[]{:S(2)}, u32[]{:S(2)}) %all-to-all-start) | async-done | bytes 262176 | tf_op jit(solution)/shard_map/all_to_all | solution.py:764
  30.7 0.1 slice.24
  30.8 0.1 copy.44
  30.9 0.1 copy.41
  31.0 0.2 convert_element_type.17
  31.2 0.6 pad_add_fusion.tile_ref
  31.8 31.9 %rows.1 = (f32[80,64,128]{2,1,0:T(8,128)}, f32[48,64,128]{2,1,0:T(8,128)}) custom-call(s32[257]{0:T(512)} %pad_add_fusion.tile_ref, f32[512,128]{1,0:T(8,128)} %bitcast.26, bf16[256,96]{1,0:T(8,128)(2,1)} %constant.69.clone.first_ref, f32[128,128]{1,0:T(8,128)} %constant.70.clone.twr_ref, f32[128,128]{1,0:T(8,128)} %constant.71.clone.twi_ref, ...), custom_call_target="tpu_custom_call" | custom-call | tf_op jit(solution)/shard_map/rows/pallas_call | solution.py:231
  63.6 62.0 %spread.1 = f32[64,2,64,128]{3,2,1,0:T(8,128)} custom-call(f32[40,2,64,128]{3,2,1,0:T(8,128)} %bitcast.24, f32[24,2,64,128]{3,2,1,0:T(8,128)} %bitcast.27), custom_call_target="tpu_custom_call" | custom-call | tf_op jit(solution)/shard_map/spread/pallas_call | solution.py:336
  125.7 33.6 %columns.1.v_ref = f32[64,256,128]{2,1,0:T(8,128)} custom-call(f32[128,64,128]{2,1,0:T(8,128)} %bitcast.21, f32[64,128,128]{2,1,0:T(8,128)} %bitcast.22, f32[64,128,128]{2,1,0:T(8,128)} %bitcast.23, bf16[256,256]{1,0:T(8,128)(2,1)} %constant.74.clone.first_ref, bf16[256,128]{1,0:T(8,128)(2,1)} %constant.75.clone.first_lo_ref, ...), custom_call_target="tpu_custom_call" | custom-call | tf_op jit(solution)/shard_map/columns/pallas_call | solution.py:433
  159.2 118.0 %back.1 = (f32[64,4096]{1,0:T(8,128)}, f32[1,128]{1,0:T(1,128)}, f32[1,128]{1,0:T(1,128)}) custom-call(f32[64,256,128]{2,1,0:T(8,128)} %columns.1.v_ref, f32[64,4096]{1,0:T(8,128)} %bitcast.28, f32[128,256]{1,0:T(8,128)} %constant.80.clone.fourth_ref, f32[128,256]{1,0:T(8,128)} %constant.81.clone.fourth_turn_ref, ...), custom_call_target="tpu_custom_call" | custom-call | tf_op jit(solution)/shard_map/back/pallas_call | solution.py:713
  277.2 1.1 slice_bitcast_fusion
  278.3 2.3 copy.46
  (7 shorter events, 0.1 us)
Async XLA Ops:
  5.7 24.9 %all-to-all-start = ((f32[64,8,128]{2,1,0:T(8,128)}), f32[64,8,128]{2,1,0:T(8,128)S(1)}, u32[]{:S(2)}, u32[]{:S(2)}) async-start(f32[64,8,128]{2,1,0:T(8,128)} %pad_maximum_fusion), calls=%async_computation | async-start | bytes 524288 | tf_op jit(solution)/shard_map/all_to_all | solution.py:764
  30.7 1.1 copy-start
